TPU v7x, 128 devices: a whole 4x4x4 slice. The times are simulated.
128 devices in a mesh: sx: 16 (over x, y_lo, core), sy: 8 (over z, y_hi).
Axes of the slice: x: 4, y: 4 (y_hi: 2, y_lo: 2; y = y_hi * 2 + y_lo), z: 4, core: 2. Of those that a mesh axis runs over, the one named last changes fastest.
Arguments:
- queries: bfloat16 [8192, 128, 128], P(('sx', 'sy')), may hold values from -8 to 8
- keys: bfloat16 [8192, 8, 128], P(('sx', 'sy')), may hold values from -8 to 8
- values: bfloat16 [8192, 8, 128], P(('sx', 'sy')), may hold values from -6 to 6
Outputs:
- attention: bfloat16 [8192, 128, 128], P(('sx', 'sy'))
All inputs are finite; a program needn't handle non-finite values.
Results may differ from a plain program's by a relative error of at most 0.005.
Values may be sent and summed in bfloat16 or wider, within the bound.
A program may use at most 64 MiB of HBM per device.

v0:
```python
import math

import jax
import jax.numpy as jnp
from jax import lax
from jax.sharding import PartitionSpec as P


def frequencies(head_width):
    half_index = jnp.arange(head_width // 2, dtype=jnp.float32)
    base_rate = jnp.power(jnp.float32(500000.0), -2.0 * half_index / head_width)
    wavelen = 2.0 * math.pi / base_rate
    smooth = (8192.0 / wavelen - 1.0) / 3.0
    blended = (1.0 - smooth) * base_rate / 8.0 + smooth * base_rate
    return jnp.where(
        wavelen < 2048.0, base_rate, jnp.where(wavelen > 8192.0, base_rate / 8.0, blended)
    )


def rotate(heads_in, positions):
    head_width = heads_in.shape[-1]
    half_width = head_width // 2
    angles = positions.astype(jnp.float32)[:, None] * frequencies(head_width)[None, :]
    cosine = jnp.cos(angles)[:, None, :]
    sine_wave = jnp.sin(angles)[:, None, :]
    widened = heads_in.astype(jnp.float32)
    front = widened[..., :half_width]
    second = widened[..., half_width:]
    turned = jnp.concatenate(
        [front * cosine - second * sine_wave, second * cosine + front * sine_wave], axis=-1
    )
    return turned.astype(jnp.bfloat16)


def attend(query_matrix, block_rows):
    total_rows, head_width = query_matrix.shape
    score_scale = 1.0 / math.sqrt(head_width)
    query_blocks = total_rows // block_rows
    offsets = jnp.arange(block_rows, dtype=jnp.int32)

    def absorb(running, gathered, start_row):
        key_piece = gathered[0][:, 0]
        value_piece = gathered[1][:, 0]
        pieces = key_piece.shape[0] // block_rows
        key_blocks = key_piece.reshape(pieces, block_rows, head_width)
        value_blocks = value_piece.reshape(pieces, block_rows, head_width)
        first_block = start_row // block_rows

        def per_query(query_index, state_now):
            row_max, row_mass, summed = state_now
            row_start = query_index * block_rows
            query_block = lax.dynamic_slice_in_dim(query_matrix, row_start, block_rows, 0)
            query_places = row_start + offsets

            def per_key(key_step, inner_state):
                block_max, block_mass, block_sum = inner_state
                key_block = lax.dynamic_index_in_dim(key_blocks, key_step, 0, keepdims=False)
                value_block = lax.dynamic_index_in_dim(value_blocks, key_step, 0, keepdims=False)
                key_places = start_row + key_step * block_rows + offsets
                scores = (
                    jnp.dot(query_block, key_block.T, preferred_element_type=jnp.float32)
                    * score_scale
                )
                scores = jnp.where(key_places[None, :] <= query_places[:, None], scores, -jnp.inf)
                new_max = jnp.maximum(block_max, jnp.max(scores, axis=1))
                shrink = jnp.exp(block_max - new_max)
                weights = jnp.exp(scores - new_max[:, None])
                block_mass = block_mass * shrink + jnp.sum(weights, axis=1)
                block_sum = block_sum * shrink[:, None] + jnp.dot(
                    weights.astype(jnp.bfloat16), value_block, preferred_element_type=jnp.float32
                )
                return (new_max, block_mass, block_sum)

            key_count = jnp.clip(query_index - first_block + 1, 0, pieces)
            inner_state = (
                lax.dynamic_slice_in_dim(row_max, row_start, block_rows, 0),
                lax.dynamic_slice_in_dim(row_mass, row_start, block_rows, 0),
                lax.dynamic_slice_in_dim(summed, row_start, block_rows, 0),
            )
            block_max, block_mass, block_sum = lax.fori_loop(0, key_count, per_key, inner_state)
            return (
                lax.dynamic_update_slice_in_dim(row_max, block_max, row_start, 0),
                lax.dynamic_update_slice_in_dim(row_mass, block_mass, row_start, 0),
                lax.dynamic_update_slice_in_dim(summed, block_sum, row_start, 0),
            )

        return lax.fori_loop(0, query_blocks, per_query, running)

    return absorb


def shards(queries, keys, values):
    local_rows, heads_all, head_width = queries.shape
    key_heads = keys.shape[1]
    group_size = heads_all // key_heads
    start_row = lax.axis_index(("sx", "sy")) * local_rows
    positions = start_row + jnp.arange(local_rows, dtype=jnp.int32)
    query_rot = rotate(queries, positions)
    key_rot = rotate(keys, positions)
    ordered = (
        query_rot.reshape(local_rows, key_heads, group_size, head_width)
        .transpose(0, 2, 1, 3)
        .reshape(local_rows, heads_all, head_width)
    )
    query_head = lax.all_to_all(ordered, ("sx", "sy"), split_axis=1, concat_axis=0, tiled=True)
    query_matrix = query_head[:, 0]
    block_rows = local_rows * lax.axis_size("sy")
    total_rows = query_matrix.shape[0]
    absorb = attend(query_matrix, block_rows)
    running = (
        jnp.full((total_rows,), -jnp.inf, jnp.float32),
        jnp.zeros((total_rows,), jnp.float32),
        jnp.zeros((total_rows, head_width), jnp.float32),
    )

    def spread(source):
        widened = jnp.broadcast_to(source[:, None], (local_rows, group_size, key_heads, head_width))
        return widened.reshape(local_rows, heads_all, head_width)

    all_keys, all_values = (
        lax.all_to_all(spread(key_rot), ("sx", "sy"), split_axis=1, concat_axis=0, tiled=True),
        lax.all_to_all(spread(values), ("sx", "sy"), split_axis=1, concat_axis=0, tiled=True),
    )
    running = absorb(running, (all_keys, all_values), jnp.zeros((), jnp.int32))
    row_max, row_mass, summed = running
    result = (summed / row_mass[:, None]).astype(jnp.bfloat16)[:, None, :]
    returned = lax.all_to_all(result, ("sx", "sy"), split_axis=0, concat_axis=1, tiled=True)
    attention = (
        returned.reshape(local_rows, group_size, key_heads, head_width)
        .transpose(0, 2, 1, 3)
        .reshape(local_rows, heads_all, head_width)
    )
    return attention


def solution(mesh):
    placed = (P(("sx", "sy"), None, None), P(("sx", "sy"), None, None), P(("sx", "sy"), None, None))
    return jax.shard_map(
        shards, mesh=mesh, in_specs=placed, out_specs=P(("sx", "sy"), None, None), check_vma=False
    )
```

profile of v0, /device:TPU:1, one launch (start us, length us, event | category | flops | bytes accessed | tf_op | source)
XLA Modules:
  0.0 505.0 jit_solution(14280930461415902531)
XLA Ops:
  0.0 4.1 convert_element_type.27
  4.3 5.0 subtract_convert_fusion
  10.5 2.7 copy.20
  13.1 11.5 %all-to-all-start = ((bf16[64,128,128]{2,0,1:T(8,128)(2,1)}), bf16[64,128,128]{2,0,1:T(8,128)(2,1)S(1)}, u32[]{:S(2)}, u32[]{:S(2)}) async-start(bf16[64,128,128]{2,0,1:T(8,128)(2,1)} %bitcast.6), calls=%async_computation | async-start | bytes 4194304 | tf_op jit(solution)/shard_map/all_to_all | solution.py:105
  25.0 30.1 %all-to-all-done = bf16[64,128,128]{2,0,1:T(8,128)(2,1)S(1)} async-done(((bf16[64,128,128]{2,0,1:T(8,128)(2,1)}), bf16[64,128,128]{2,0,1:T(8,128)(2,1)S(1)}, u32[]{:S(2)}, u32[]{:S(2)}) %all-to-all-start) | async-done | bytes 2097184 | tf_op jit(solution)/shard_map/all_to_all | solution.py:105
  55.1 2.0 broadcast_in_dim.18
  57.2 7.2 %all-to-all-start.1 = ((bf16[64,128,128]{2,0,1:T(8,128)(2,1)}), bf16[64,128,128]{2,0,1:T(8,128)(2,1)}, u32[]{:S(2)}, u32[]{:S(2)}) async-start(bf16[64,128,128]{2,0,1:T(8,128)(2,1)} %bitcast.10), calls=%async_computation.1 | async-start | bytes 4194304 | tf_op jit(solution)/shard_map/all_to_all | solution.py:121
  64.4 30.1 %all-to-all-done.1 = bf16[64,128,128]{2,0,1:T(8,128)(2,1)} async-done(((bf16[64,128,128]{2,0,1:T(8,128)(2,1)}), bf16[64,128,128]{2,0,1:T(8,128)(2,1)}, u32[]{:S(2)}, u32[]{:S(2)}) %all-to-all-start.1) | async-done | bytes 2097184 | tf_op jit(solution)/shard_map/all_to_all | solution.py:121
  94.5 1.9 broadcast_in_dim.19
  96.4 6.5 %all-to-all-start.2 = ((bf16[64,128,128]{2,0,1:T(8,128)(2,1)}), bf16[64,128,128]{2,0,1:T(8,128)(2,1)S(1)}, u32[]{:S(2)}, u32[]{:S(2)}) async-start(bf16[64,128,128]{2,0,1:T(8,128)(2,1)} %bitcast.53), calls=%async_computation.2 | async-start | bytes 4194304 | tf_op jit(solution)/shard_map/all_to_all | solution.py:122
  102.8 30.5 %all-to-all-done.2 = bf16[64,128,128]{2,0,1:T(8,128)(2,1)S(1)} async-done(((bf16[64,128,128]{2,0,1:T(8,128)(2,1)}), bf16[64,128,128]{2,0,1:T(8,128)(2,1)S(1)}, u32[]{:S(2)}, u32[]{:S(2)}) %all-to-all-start.2) | async-done | bytes 2097184 | tf_op jit(solution)/shard_map/all_to_all | solution.py:122
  133.3 2.2 broadcast_in_dim.17
  135.5 310.3 %while.67 = (s32[]{:T(128)}, f32[8192]{0:T(1024)S(1)}, f32[8192]{0:T(1024)S(1)}, f32[8192,128]{1,0:T(8,128)}, bf16[8192,128]{1,0:T(8,128)(2,1)}, /*index=5*/bf16...) while((s32[]{:T(128)}, f32[8192]{0:T(1024)S(1)}, ...), condition=%wide.region_5.6_spmd.clone.clone, body=%wide.region_0.5_spmd.clone.clone.sunk | while | flops 136448000 | bytes 5435970 | solution.py:87
  137.6 1.9 while.68
  137.6 1.2 fusion.25
  142.8 3.8 while.68
  149.9 5.7 %while.68 = (s32[]{:T(128)}, f32[512]{0:T(512)S(1)}, f32[512]{0:T(512)S(1)}, f32[512,128]{1,0:T(8,128)S(1)}, s32[]{:T(128)}, /*index=5*/s32[512]{0:T(512)S(1)}, ...) while((s32[]{:T(128)}, f32[512]{0:T(512)S(1)}, ...), condition=%wide.region_4.4_spmd, body=%wide.region_1.3_spmd.sunk | while | flops 136447488 | bytes 4104391 | solution.py:80
  150.0 1.2 fusion.25
  158.9 7.6 %while.68 = (s32[]{:T(128)}, f32[512]{0:T(512)S(1)}, f32[512]{0:T(512)S(1)}, f32[512,128]{1,0:T(8,128)S(1)}, s32[]{:T(128)}, /*index=5*/s32[512]{0:T(512)S(1)}, ...) while((s32[]{:T(128)}, f32[512]{0:T(512)S(1)}, ...), condition=%wide.region_4.4_spmd, body=%wide.region_1.3_spmd.sunk | while | flops 136447488 | bytes 4104391 | solution.py:80
  159.0 1.2 fusion.25
  169.8 9.5 %while.68 = (s32[]{:T(128)}, f32[512]{0:T(512)S(1)}, f32[512]{0:T(512)S(1)}, f32[512,128]{1,0:T(8,128)S(1)}, s32[]{:T(128)}, /*index=5*/s32[512]{0:T(512)S(1)}, ...) while((s32[]{:T(128)}, f32[512]{0:T(512)S(1)}, ...), condition=%wide.region_4.4_spmd, body=%wide.region_1.3_spmd.sunk | while | flops 136447488 | bytes 4104391 | solution.py:80
  177.4 1.2 fusion.25
  182.6 11.4 %while.68 = (s32[]{:T(128)}, f32[512]{0:T(512)S(1)}, f32[512]{0:T(512)S(1)}, f32[512,128]{1,0:T(8,128)S(1)}, s32[]{:T(128)}, /*index=5*/s32[512]{0:T(512)S(1)}, ...) while((s32[]{:T(128)}, f32[512]{0:T(512)S(1)}, ...), condition=%wide.region_4.4_spmd, body=%wide.region_1.3_spmd.sunk | while | flops 136447488 | bytes 4104391 | solution.py:80
  190.2 1.2 fusion.25
  197.3 13.2 %while.68 = (s32[]{:T(128)}, f32[512]{0:T(512)S(1)}, f32[512]{0:T(512)S(1)}, f32[512,128]{1,0:T(8,128)S(1)}, s32[]{:T(128)}, /*index=5*/s32[512]{0:T(512)S(1)}, ...) while((s32[]{:T(128)}, f32[512]{0:T(512)S(1)}, ...), condition=%wide.region_4.4_spmd, body=%wide.region_1.3_spmd.sunk | while | flops 136447488 | bytes 4104391 | solution.py:80
  203.0 1.2 fusion.25
  213.8 15.1 %while.68 = (s32[]{:T(128)}, f32[512]{0:T(512)S(1)}, f32[512]{0:T(512)S(1)}, f32[512,128]{1,0:T(8,128)S(1)}, s32[]{:T(128)}, /*index=5*/s32[512]{0:T(512)S(1)}, ...) while((s32[]{:T(128)}, f32[512]{0:T(512)S(1)}, ...), condition=%wide.region_4.4_spmd, body=%wide.region_1.3_spmd.sunk | while | flops 136447488 | bytes 4104391 | solution.py:80
  213.9 1.2 fusion.25
  225.2 1.2 fusion.25
  232.3 17.0 %while.68 = (s32[]{:T(128)}, f32[512]{0:T(512)S(1)}, f32[512]{0:T(512)S(1)}, f32[512,128]{1,0:T(8,128)S(1)}, s32[]{:T(128)}, /*index=5*/s32[512]{0:T(512)S(1)}, ...) while((s32[]{:T(128)}, f32[512]{0:T(512)S(1)}, ...), condition=%wide.region_4.4_spmd, body=%wide.region_1.3_spmd.sunk | while | flops 136447488 | bytes 4104391 | solution.py:80
  234.2 1.2 fusion.25
  236.1 1.2 fusion.25
  238.0 1.2 fusion.25
  252.6 18.9 %while.68 = (s32[]{:T(128)}, f32[512]{0:T(512)S(1)}, f32[512]{0:T(512)S(1)}, f32[512,128]{1,0:T(8,128)S(1)}, s32[]{:T(128)}, /*index=5*/s32[512]{0:T(512)S(1)}, ...) while((s32[]{:T(128)}, f32[512]{0:T(512)S(1)}, ...), condition=%wide.region_4.4_spmd, body=%wide.region_1.3_spmd.sunk | while | flops 136447488 | bytes 4104391 | solution.py:80
  252.7 1.2 fusion.25
  274.9 20.8 %while.68 = (s32[]{:T(128)}, f32[512]{0:T(512)S(1)}, f32[512]{0:T(512)S(1)}, f32[512,128]{1,0:T(8,128)S(1)}, s32[]{:T(128)}, /*index=5*/s32[512]{0:T(512)S(1)}, ...) while((s32[]{:T(128)}, f32[512]{0:T(512)S(1)}, ...), condition=%wide.region_4.4_spmd, body=%wide.region_1.3_spmd.sunk | while | flops 136447488 | bytes 4104391 | solution.py:80
  299.0 22.7 %while.68 = (s32[]{:T(128)}, f32[512]{0:T(512)S(1)}, f32[512]{0:T(512)S(1)}, f32[512,128]{1,0:T(8,128)S(1)}, s32[]{:T(128)}, /*index=5*/s32[512]{0:T(512)S(1)}, ...) while((s32[]{:T(128)}, f32[512]{0:T(512)S(1)}, ...), condition=%wide.region_4.4_spmd, body=%wide.region_1.3_spmd.sunk | while | flops 136447488 | bytes 4104391 | solution.py:80
  325.1 24.6 %while.68 = (s32[]{:T(128)}, f32[512]{0:T(512)S(1)}, f32[512]{0:T(512)S(1)}, f32[512,128]{1,0:T(8,128)S(1)}, s32[]{:T(128)}, /*index=5*/s32[512]{0:T(512)S(1)}, ...) while((s32[]{:T(128)}, f32[512]{0:T(512)S(1)}, ...), condition=%wide.region_4.4_spmd, body=%wide.region_1.3_spmd.sunk | while | flops 136447488 | bytes 4104391 | solution.py:80
  353.0 26.5 %while.68 = (s32[]{:T(128)}, f32[512]{0:T(512)S(1)}, f32[512]{0:T(512)S(1)}, f32[512,128]{1,0:T(8,128)S(1)}, s32[]{:T(128)}, /*index=5*/s32[512]{0:T(512)S(1)}, ...) while((s32[]{:T(128)}, f32[512]{0:T(512)S(1)}, ...), condition=%wide.region_4.4_spmd, body=%wide.region_1.3_spmd.sunk | while | flops 136447488 | bytes 4104391 | solution.py:80
  382.8 28.4 %while.68 = (s32[]{:T(128)}, f32[512]{0:T(512)S(1)}, f32[512]{0:T(512)S(1)}, f32[512,128]{1,0:T(8,128)S(1)}, s32[]{:T(128)}, /*index=5*/s32[512]{0:T(512)S(1)}, ...) while((s32[]{:T(128)}, f32[512]{0:T(512)S(1)}, ...), condition=%wide.region_4.4_spmd, body=%wide.region_1.3_spmd.sunk | while | flops 136447488 | bytes 4104391 | solution.py:80
  414.4 30.2 %while.68 = (s32[]{:T(128)}, f32[512]{0:T(512)S(1)}, f32[512]{0:T(512)S(1)}, f32[512,128]{1,0:T(8,128)S(1)}, s32[]{:T(128)}, /*index=5*/s32[512]{0:T(512)S(1)}, ...) while((s32[]{:T(128)}, f32[512]{0:T(512)S(1)}, ...), condition=%wide.region_4.4_spmd, body=%wide.region_1.3_spmd.sunk | while | flops 136447488 | bytes 4104391 | solution.py:80
  445.8 2.9 fusion.14
  449.2 2.8 reduce
  452.0 3.9 reshape.125
  455.9 37.2 %all_to_all.60 = bf16[128,2,4096]{2,1,0:T(2,128)(2,1)S(1)} all-to-all(bf16[128,2,4096]{2,1,0:T(2,128)(2,1)} %reshape.125), channel_id=1, replica_groups=mesh['sx'=16,'sy'=8] {'sx','sy'}, dimensions={0} | all-to-all | bytes 4194304 | tf_op jit(solution)/shard_map/all_to_all | solution.py:127
  493.2 6.7 %reshape.126 = bf16[8192,1,128]{2,1,0:T(2,128)(2,1)} reshape(bf16[128,2,4096]{2,1,0:T(2,128)(2,1)S(1)} %all_to_all.60) | data formatting | bytes 4194304
  499.9 2.5 copy.27
  502.3 2.7 copy.25
  (1102 shorter events, 291.1 us)
Async XLA Ops:
  13.1 11.5 %copy-start.1 = (bf16[64,8,128]{2,1,0:T(8,128)(2,1)S(1)}, bf16[64,8,128]{2,1,0:T(8,128)(2,1)}, u32[]{:S(2)}) copy-start(bf16[64,8,128]{2,1,0:T(8,128)(2,1)} %param.8) | copy-start | bytes 393220
  13.1 42.0 %all-to-all-start = ((bf16[64,128,128]{2,0,1:T(8,128)(2,1)}), bf16[64,128,128]{2,0,1:T(8,128)(2,1)S(1)}, u32[]{:S(2)}, u32[]{:S(2)}) async-start(bf16[64,128,128]{2,0,1:T(8,128)(2,1)} %bitcast.6), calls=%async_computation | async-start | bytes 4194304 | tf_op jit(solution)/shard_map/all_to_all | solution.py:105
  55.1 2.0 copy-start
  57.1 7.3 %copy-start.2 = (bf16[64,8,128]{2,1,0:T(8,128)(2,1)S(1)}, bf16[64,8,128]{2,1,0:T(8,128)(2,1)}, u32[]{:S(2)}) copy-start(bf16[64,8,128]{2,1,0:T(8,128)(2,1)} %param.9) | copy-start | bytes 393220
  57.2 37.4 %all-to-all-start.1 = ((bf16[64,128,128]{2,0,1:T(8,128)(2,1)}), bf16[64,128,128]{2,0,1:T(8,128)(2,1)}, u32[]{:S(2)}, u32[]{:S(2)}) async-start(bf16[64,128,128]{2,0,1:T(8,128)(2,1)} %bitcast.10), calls=%async_computation.1 | async-start | bytes 4194304 | tf_op jit(solution)/shard_map/all_to_all | solution.py:121
  96.4 36.9 %all-to-all-start.2 = ((bf16[64,128,128]{2,0,1:T(8,128)(2,1)}), bf16[64,128,128]{2,0,1:T(8,128)(2,1)S(1)}, u32[]{:S(2)}, u32[]{:S(2)}) async-start(bf16[64,128,128]{2,0,1:T(8,128)(2,1)} %bitcast.53), calls=%async_computation.2 | async-start | bytes 4194304 | tf_op jit(solution)/shard_map/all_to_all | solution.py:122
where the time goes:
time: 510 us; the launch traced here: 505 us
  matrix products  221 us (43%)
  waiting for transfers between devices  90.6 us (18%)
  local copies, waits for them, and re-layouts  77.7 us (15%)
  other arithmetic  46.4 us (9%)
  blocking collectives  37.2 us (7%)
  starting transfers between devices  25.2 us (5%)
  loops' own time  6.72 us (1%)
    dot_general x136, matrix products, per_key(): jnp.dot(query_block, key_block.T, preferred_element_type=jnp.float32)  167 us
    dot_general x136, matrix products, per_key(): jnp.dot(weights.astype(jnp.bfloat16), value_block, preferred_element_type...  53.8 us
    all_to_all x1, blocking collectives, shards(): lax.all_to_all(result, ('sx', 'sy'), split_axis=0, concat_axis=1, tiled=T...  37.2 us
    all_to_all x1, waiting for transfers between devices, shards(): lax.all_to_all(spread(values), ('sx', 'sy'), split_axis=1, concat_axis=0,...  30.5 us
    all_to_all x1, waiting for transfers between devices, shards(): lax.all_to_all(ordered, ('sx', 'sy'), split_axis=1, concat_axis=0, tiled=...  30.1 us
    all_to_all x1, waiting for transfers between devices, shards(): lax.all_to_all(spread(key_rot), ('sx', 'sy'), split_axis=1, concat_axis=0...  30.1 us
    reduce_sum x136, other arithmetic, per_key(): block_mass = block_mass * shrink + jnp.sum(weights, axis=1)  26.7 us
    dynamic_slice x16, local copies, waits for them, and re-layouts, per_query(): lax.dynamic_slice_in_dim(summed, row_start, block_rows, 0)  15.5 us
  transfers between devices with their start and end apart: 3, of which 3 were waited for; matrix products, arithmetic and copies ran while one was open for 0% of the time, Pallas kernels for 0%

commit v1 on v0

v1 whole, which is shorter than its diff:
```python
import functools
import math

import jax
import jax.numpy as jnp
from jax import lax
from jax.experimental import pallas as pl
from jax.experimental.pallas import tpu as pltpu
from jax.sharding import PartitionSpec as P

MESH = pl.DeviceIdType.MESH
F32 = jnp.float32
BF16 = jnp.bfloat16
NEG = -1e30
CW = 256
QW = 1024
KB = 512
VR = 144
UNITS = 68
SCALE = math.log2(math.e) / math.sqrt(128.0)


def frequencies(head_width):
    half_index = jnp.arange(head_width // 2, dtype=F32)
    base_rate = jnp.power(F32(500000.0), -2.0 * half_index / head_width)
    wavelen = 2.0 * math.pi / base_rate
    smooth = (8192.0 / wavelen - 1.0) / 3.0
    blended = (1.0 - smooth) * base_rate / 8.0 + smooth * base_rate
    return jnp.where(
        wavelen < 2048.0, base_rate, jnp.where(wavelen > 8192.0, base_rate / 8.0, blended)
    )


def place(p, b):
    return jnp.where(b == 0, p, 3 - p)


class Spot:
    def __init__(self, p, b, core):
        self.p, self.b, self.core = tuple(p), tuple(b), core

    @staticmethod
    def own():
        sx, sy = lax.axis_index("sx"), lax.axis_index("sy")
        xyz = (sx // 4, (sy % 2) * 2 + (sx // 2) % 2, sy // 2)
        return Spot([((c + 1) // 2) % 2 for c in xyz], [c // 2 for c in xyz], sx % 2)

    @property
    def sx(self):
        ylo = (self.p[1] + self.b[1]) % 2
        return place(self.p[0], self.b[0]) * 4 + ylo * 2 + self.core

    @property
    def sy(self):
        return place(self.p[2], self.b[2]) * 2 + self.b[1]

    @property
    def device(self):
        return (self.sx, self.sy)

    @property
    def chip(self):
        return self.b[0] * 4 + self.b[1] * 2 + self.b[2]

    @property
    def head_block(self):
        return self.chip * 2 + self.core

    @property
    def pair_block(self):
        return (self.b[0] * 2 + self.b[1]) * 2 + self.core

    @property
    def slot(self):
        return self.pair_block * 2 + self.b[2]

    @property
    def part(self):
        return self.p[1] * 2 + self.p[2]

    def member(self, d, dc):
        return Spot(self.p, [(b + (d >> s) % 2) % 2 for b, s in zip(self.b, (2, 1, 0))], (self.core + dc) % 2)

    def cousin(self, d):
        return Spot([(p + (d >> s) % 2) % 2 for p, s in zip(self.p, (2, 1, 0))], self.b, self.core)


ORDER = (7, 3, 5, 6, 1, 2, 4, 0)


def kernel(q_ref, kv_ref, cos_ref, sin_ref, out_ref,
           qs, qr, kvb, ost, qT, vT, s0, s1, s2, s3, p0, p1, p2, p3, mx, al, m_ref, acc_ref,
           q_send, q_recv, k1_send, k1_recv, k2_send, k2_recv, f_send, f_recv, o_send, o_recv):
    S, W = (s0, s1, s2, s3), (p0, p1, p2, p3)
    H = CW // 128
    me = Spot.own()
    others = [(d, dc) for d in ORDER for dc in (1, 0) if (d, dc) != (0, 0)]

    def remote(src, dst, send, recv, spot):
        return pltpu.make_async_remote_copy(src_ref=src, dst_ref=dst, send_sem=send, recv_sem=recv, device_id=spot.device, device_id_type=MESH)

    barrier = pltpu.get_barrier_semaphore()
    for d, dc in others:
        pl.semaphore_signal(barrier, inc=1, device_id=me.member(d, dc).device, device_id_type=MESH)
    for d in range(1, 8):
        pl.semaphore_signal(barrier, inc=1, device_id=me.cousin(d).device, device_id_type=MESH)
    pl.semaphore_wait(barrier, len(others) + 7)

    def kv_spot(role, src):
        return kvb.at[role, src.sx, src.part, pl.ds(pl.multiple_of(src.b[2] * 64, 64), 64), :]

    def first(d, dc):
        to = me.member(d, dc)
        return remote(kv_ref.at[to.core, to.chip], kv_spot(to.core, me), k1_send.at[d * 2 + dc], k1_recv.at[me.slot], to)

    for d, dc in others:
        first(d, dc).start()
    kvb[me.core, me.sx, me.part, pl.ds(pl.multiple_of(me.b[2] * 64, 64), 64), :] = kv_ref[me.core, me.chip]

    def queries_to(d, dc):
        to = me.member(d, dc)
        return remote(qs.at[to.head_block], qr.at[me.slot], q_send.at[d * 2 + dc], q_recv.at[me.slot], to)

    for d in ORDER:
        to = me.member(d, 0)
        x = q_ref[:, pl.ds(pl.multiple_of(to.chip * 16, 16), 16), :].astype(F32)
        for c in range(2):
            part = x[:, c * 8:(c + 1) * 8, :].reshape(512, 128)
            turned = part * cos_ref[...] + pltpu.roll(part, 64, 1) * sin_ref[...]
            qs[to.chip * 2 + c] = turned.astype(BF16)
        for dc in (1, 0):
            if (d, dc) != (0, 0):
                queries_to(d, dc).start()
    qr[me.slot] = qs[me.head_block]

    for d, dc in others:
        frm = me.member(d, dc)
        remote(kv_ref.at[0, 0], kv_spot(me.core, frm), k1_send.at[d * 2 + dc], k1_recv.at[frm.slot], frm).wait_recv()

    def region(spot, half):
        return kvb.at[me.core, pl.ds(pl.multiple_of(place(spot.p[0], half) * 4, 4), 4), spot.part]

    def second(d, half):
        r = region(me, half)
        return remote(r, r, k2_send.at[d * 2 + half], k2_recv.at[d * 2 + half], me.cousin(d))

    def forward(d, half):
        r = region(me.cousin(d), half)
        return remote(r, r, f_send.at[d * 2 + half], f_recv.at[d * 2 + half], me.member(0, 1))

    for d in (7, 3, 5, 6, 1, 2, 4):
        for half in range(2):
            second(d, half).start()
    for half in range(2):
        forward(0, half).start()
    for d in (4, 2, 1, 6, 5, 3, 7):
        for half in range(2):
            r = region(me.cousin(d), half)
            remote(r, r, k2_send.at[d * 2 + half], k2_recv.at[d * 2 + half], me.cousin(d)).wait_recv()
            forward(d, half).start()
    for d in range(8):
        for half in range(2):
            other = kvb.at[1 - me.core, pl.ds(pl.multiple_of(place(me.cousin(d).p[0], half) * 4, 4), 4), me.cousin(d).part]
            remote(other, other, f_send.at[d * 2 + half], f_recv.at[d * 2 + half], me.member(0, 1)).wait_recv()
    for d, dc in others:
        frm = me.member(d, dc)
        remote(qs.at[0], qr.at[frm.slot], q_send.at[d * 2 + dc], q_recv.at[frm.slot], frm).wait_recv()

    @pl.loop(0, 8)
    def _(i):
        for t in range(QW // 256):
            x = qr[2 * i + t // 2, pl.ds((t % 2) * 256, 256), :].astype(F32) * SCALE
            xt = x.T
            hi = xt.astype(BF16)
            lo = (xt - hi.astype(F32)).astype(BF16)
            for h in range(2):
                qT[i, 2 * t + h, 0:128, :] = hi[:, h * 128:(h + 1) * 128]
                qT[i, 2 * t + h, 128:256, :] = lo[:, h * 128:(h + 1) * 128]

    @pl.loop(0, 16)
    def _(b):
        for h in range(4):
            vT[b, h, 0:128, :] = kvb[1, b, h].T
            vT[b, h, 128:VR, :] = jnp.ones((VR - 128, 128), BF16)

    m_ref[...] = jnp.full_like(m_ref, NEG)
    acc_ref[...] = jnp.zeros_like(acc_ref)
    al[...] = jnp.zeros_like(al)
    for w in W[2:]:
        w[...] = jnp.zeros_like(w)

    i0 = me.pair_block

    def blk(j):
        return (i0 + j) % 8

    def source(i, bz):
        return Spot(me.p, (i // 4, (i // 2) % 2, bz), i % 2)

    def last_of(j):
        return source(blk(j), 0).sx

    def adv(u):
        j, b = u
        last = b == last_of(j)
        return jnp.minimum(jnp.where(last, j + 1, j), 7), jnp.where(last, 0, b + 1)

    def qk_stage(u, slot):
        j, b = u
        i = blk(j)
        for n in range(QW // CW):
            cols = pl.ds(n * CW, CW)
            kb = kvb[0, b].reshape(KB, 128)
            kk = jnp.concatenate([kb, kb], axis=1)
            qq = jnp.concatenate([qT[i, n * H + h] for h in range(H)], axis=1)
            s = jnp.dot(kk, qq, preferred_element_type=F32)
            S[slot][:, cols] = s
            mx[slot, :, cols] = jnp.max(s, axis=0, keepdims=True)

    def mask(u, slot):
        j, b = u

        @pl.loop(0, jnp.where(b == last_of(j), 1, 0))
        def _(_):
            here = source(blk(j), 0)
            ylo = (here.p[1] + here.b[1]) % 2
            row = lax.broadcasted_iota(jnp.int32, (KB, 128), 0)
            ky_hi = (row // 256 + ylo) % 2
            kpz, kbz = (row // 128) % 2, (row // 64) % 2
            key_at = (jnp.where(kbz == 0, kpz, 3 - kpz) * 2 + ky_hi) * 64 + row % 64
            for n in range(QW // 128):
                cols = pl.ds(n * 128, 128)
                col = lax.broadcasted_iota(jnp.int32, (KB, 128), 1) + (n % 4) * 128
                query_at = source(blk(j), n // 4).sy * 64 + col // 8
                s = jnp.where(key_at <= query_at, S[slot][:, cols], NEG)
                S[slot][:, cols] = s
                mx[slot, :, cols] = jnp.max(s, axis=0, keepdims=True)

    def soft_stage(u, slot):
        j, b = u
        m_old = jnp.where(b == 0, NEG, m_ref[...])
        m_new = jnp.maximum(m_old, mx[slot])
        m_ref[...] = m_new
        al[slot] = jnp.exp2(m_old - m_new)
        for n in range(QW // CW):
            cols = pl.ds(n * CW, CW)
            w = jnp.exp2(S[slot][:, cols] - m_new[:, n * CW:(n + 1) * CW]).astype(BF16)
            for h in range(H):
                W[slot][n * H + h] = w[:, h * 128:(h + 1) * 128]

    def pv_stage(u, slot):
        j, b = u
        par = j % 2
        for n in range(QW // CW):
            cols = pl.ds(n * CW, CW)
            ww = jnp.concatenate([W[slot][n * H + h] for h in range(H)], axis=1)
            vv = jnp.concatenate([vT[b, h] for h in range(4)], axis=1)
            acc_ref[par, :, cols] = acc_ref[par, :, cols] * al[slot, :, cols] + jnp.dot(vv, ww, preferred_element_type=F32)

    def outputs_to(s):
        to = Spot(me.p, (s // 8, (s // 4) % 2, s % 2), (s // 2) % 2)
        heads = pl.ds(pl.multiple_of(me.head_block * 8, 8), 8)
        return remote(ost.at[s], out_ref.at[:, heads, :], o_send.at[s], o_recv.at[me.head_block], to)

    def fin(u):
        j, b = u

        @pl.loop(0, jnp.where(b == last_of(j), 1, 0))
        def _(_):
            i = blk(j)
            par = j % 2
            o = acc_ref[par, 0:128, :] * (1.0 / acc_ref[par, 128:129, :])
            for bz in range(2):
                s = 2 * i + bz
                for t in range(2):
                    c0 = bz * 512 + t * 256
                    ost[s, pl.ds(t * 32, 32)] = o[:, c0:c0 + 256].T.reshape(32, 8, 128).astype(BF16)

                @pl.when(s != me.slot)
                def _():
                    outputs_to(s).start()

                @pl.when(s == me.slot)
                def _():
                    out_ref[:, pl.ds(pl.multiple_of(me.head_block * 8, 8), 8), :] = ost[s]

    z = jnp.int32(0)
    u0 = (z, z)
    u1 = adv(u0)
    qk_stage(u0, 0)
    qk_stage(u1, 1)
    mask(u0, 0)
    mask(u1, 1)

    def step(carry, cur, nxt):
        pa, pb, ca, cb, na, nb = carry
        qk_stage(na, nxt)
        qk_stage(nb, nxt + 1)
        soft_stage(ca, cur)
        soft_stage(cb, cur + 1)
        pv_stage(pa, nxt)
        pv_stage(pb, nxt + 1)
        mask(na, nxt)
        mask(nb, nxt + 1)
        fin(pa)
        fin(pb)
        n2 = adv(nb)
        return ca, cb, na, nb, n2, adv(n2)

    dummy = (z, jnp.where(last_of(z) == 0, 1, 0))
    u2 = adv(u1)
    carry = (dummy, dummy, u0, u1, u2, adv(u2))
    carry = lax.fori_loop(0, UNITS // 4, lambda _, c: step(step(c, 0, 2), 2, 0), carry)
    pv_stage(carry[0], 2)
    pv_stage(carry[1], 3)
    fin(carry[0])
    fin(carry[1])

    for d, dc in others:
        first(d, dc).wait_send()
        queries_to(d, dc).wait_send()
        frm = me.member(d, dc)
        outputs_to(frm.slot).wait_send()
        heads = pl.ds(pl.multiple_of(frm.head_block * 8, 8), 8)
        remote(ost.at[0], out_ref.at[:, heads, :], o_send.at[frm.slot], o_recv.at[frm.head_block], frm).wait_recv()
    for d in range(8):
        for half in range(2):
            forward(d, half).wait_send()
            if d:
                second(d, half).wait_send()


def shards(queries, keys, values):
    rows, heads, width = queries.shape
    start = lax.axis_index(("sx", "sy")) * rows
    positions = start + jnp.arange(rows, dtype=jnp.int32)
    angles = positions.astype(F32)[:, None] * frequencies(width)[None, :]
    cosine, sine = jnp.cos(angles), jnp.sin(angles)
    cos2 = jnp.concatenate([cosine, cosine], axis=1)
    sin2 = jnp.concatenate([-sine, sine], axis=1)
    wide = keys.astype(F32)
    turned = wide * cos2[:, None, :] + jnp.roll(wide, width // 2, axis=2) * sin2[:, None, :]
    kv = jnp.stack([turned.astype(BF16).transpose(1, 0, 2), values.transpose(1, 0, 2)])

    def eightfold(a):
        return jnp.broadcast_to(a[:, None, :], (rows, 8, width)).reshape(rows * 8, width)

    dma = pltpu.SemaphoreType.DMA
    return pl.pallas_call(
        kernel,
        out_shape=jax.ShapeDtypeStruct((rows, heads, width), BF16),
        in_specs=[pl.BlockSpec(memory_space=pltpu.VMEM)] * 4,
        out_specs=pl.BlockSpec(memory_space=pltpu.VMEM),
        scratch_shapes=[
            pltpu.VMEM((16, 512, 128), BF16),
            pltpu.VMEM((16, 512, 128), BF16),
            pltpu.VMEM((2, 16, 4, 128, 128), BF16),
            pltpu.VMEM((16, 64, 8, 128), BF16),
            pltpu.VMEM((8, 8, 256, 128), BF16),
            pltpu.VMEM((16, 4, VR, 128), BF16),
            *[pltpu.VMEM((KB, QW), F32)] * 4,
            *[pltpu.VMEM((8, KB, 128), BF16)] * 4,
            pltpu.VMEM((4, 1, QW), F32),
            pltpu.VMEM((4, 1, QW), F32),
            pltpu.VMEM((1, QW), F32),
            pltpu.VMEM((2, VR, QW), F32),
            *[dma((16,))] * 10,
        ],
        compiler_params=pltpu.CompilerParams(
            collective_id=0, has_side_effects=True, vmem_limit_bytes=58 << 20
        ),
        name="fused",
    )(queries, kv, eightfold(cos2), eightfold(sin2))


def solution(mesh):
    placed = P(("sx", "sy"), None, None)
    return jax.shard_map(
        shards, mesh=mesh, in_specs=(placed, placed, placed), out_specs=placed, check_vma=False
    )
```

time: 510 us -> 128 us (0.25)
  matrix products: 221 us -> 0 us
  Pallas kernels: 0 us -> 120 us
  waiting for transfers between devices: 90.6 us -> 0 us
  local copies, waits for them, and re-layouts: 77.7 us -> 5.67 us
  other arithmetic: 46.4 us -> 2.11 us
  blocking collectives: 37.2 us -> 0 us
  starting transfers between devices: 25.2 us -> 0 us
  loops' own time: 6.72 us -> 0 us
    dot_general x272 -> x0, matrix products: 221 us -> none  [the longest x136 167 us: per_key(): jnp.dot(query_block, key_block.T, preferred_element_type=jnp.float32)]
    pallas_call x0 -> x1, Pallas kernels: none -> 120 us  [shards(): pl.pallas_call(kernel, out_shape=jax.ShapeDtypeStruct((rows, heads, width...]
    all_to_all x3 -> x0, waiting for transfers between devices: 90.6 us -> none  [the longest x1 30.5 us: shards(): lax.all_to_all(spread(values), ('sx', 'sy'), split_axis=1, concat_axis=0,...]
    all_to_all x1 -> x0, blocking collectives: 37.2 us -> none  [shards(): lax.all_to_all(result, ('sx', 'sy'), split_axis=0, concat_axis=1, tiled=T...]
    dynamic_slice x64 -> x0, local copies, waits for them, and re-layouts: 32.6 us -> none  [the longest x16 15.5 us: per_query(): lax.dynamic_slice_in_dim(summed, row_start, block_rows, 0)]
    reduce_sum x136 -> x0, other arithmetic: 26.7 us -> none  [per_key(): block_mass = block_mass * shrink + jnp.sum(weights, axis=1)]
    all_to_all x3 -> x0, starting transfers between devices: 25.2 us -> none  [the longest x1 11.5 us: shards(): lax.all_to_all(ordered, ('sx', 'sy'), split_axis=1, concat_axis=0, tiled=...]
    dynamic_update_slice x48 -> x0, local copies, waits for them, and re-layouts: 19.8 us -> none  [the longest x16 11.4 us: per_query(): lax.dynamic_update_slice_in_dim(summed, block_sum, row_start, 0)]
  transfers between devices with their start and end apart: 3 -> 0, of which waited for: 3 -> 0; matrix products, arithmetic and copies ran while one was open for 0% -> 0% of each run, Pallas kernels for 0% -> 0%
where the time goes in v1:
time: 128 us
  Pallas kernels  120 us (94%)
  local copies, waits for them, and re-layouts  5.67 us (4%)
  other arithmetic  2.11 us (2%)
    pallas_call x1, Pallas kernels, shards(): pl.pallas_call(kernel, out_shape=jax.ShapeDtypeStruct((rows, heads, width...  120 us
    unnamed x4, local copies, waits for them, and re-layouts  4.09 us

profile of v1, /device:TPU:1, one launch (start us, length us, event | category | flops | bytes accessed | tf_op | source)
XLA Modules:
  0.0 127.6 jit_solution(822451193349466707)
XLA Ops:
  0.0 0.0 copy-start
  0.0 0.2 multiply_cosine_fusion
  0.2 0.1 pad_maximum_fusion.1
  0.3 0.9 copy.14
  1.3 0.7 broadcast_bitcast_fusion.1.cos_ref
  2.0 0.7 broadcast_bitcast_fusion.sin_ref
  2.7 0.9 copy_convert_fusion
  3.6 0.1 fusion.4
  3.8 0.0 copy-done
  3.8 0.1 fusion.2
  3.9 0.7 pad_maximum_fusion.kv_ref
  4.7 119.8 %fused.1 = bf16[64,128,128]{2,1,0:T(8,128)(2,1)} custom-call(bf16[64,128,128]{2,1,0:T(8,128)(2,1)} %q_ref.1, bf16[2,8,64,128]{3,2,1,0:T(8,128)(2,1)} %pad_maximum_fusion.kv_ref, f32[512,128]{1,0:T(8,128)} %broadcast_bitcast_fusion.1.cos_ref, f32[512,128]{1,0:T(8,128)} %broadcast_bitcast_fusion.sin_ref), custom_call_target="tpu_custom_call" | custom-call | tf_op jit(solution)/shard_map/fused/pallas_call | solution.py:349
  124.4 3.2 %copy.16 = bf16[64,128,128]{2,1,0:T(8,128)(2,1)} copy(bf16[64,128,128]{2,1,0:T(8,128)(2,1)} %fused.1) | data formatting | bytes 4194304
  (2 shorter events, 0.0 us)
Async XLA Ops:
  0.0 3.8 %copy-start = (bf16[64,8,128]{2,1,0:T(8,128)(2,1)S(1)}, bf16[64,8,128]{2,1,0:T(8,128)(2,1)}, u32[]{:S(2)}) copy-start(bf16[64,8,128]{2,1,0:T(8,128)(2,1)} %param.4) | copy-start | bytes 393220

commit v2 on v1

v2 whole, which is shorter than its diff:
```python
import functools
import math

import jax
import jax.numpy as jnp
from jax import lax
from jax.experimental import pallas as pl
from jax.experimental.pallas import tpu as pltpu
from jax.sharding import PartitionSpec as P

MESH = pl.DeviceIdType.MESH
F32 = jnp.float32
BF16 = jnp.bfloat16
NEG = -1e30
CW = 256
QW = 1024
KB = 512
VR = 144
SCALE = math.log2(math.e) / math.sqrt(128.0)


def frequencies(head_width):
    half_index = jnp.arange(head_width // 2, dtype=F32)
    base_rate = jnp.power(F32(500000.0), -2.0 * half_index / head_width)
    wavelen = 2.0 * math.pi / base_rate
    smooth = (8192.0 / wavelen - 1.0) / 3.0
    blended = (1.0 - smooth) * base_rate / 8.0 + smooth * base_rate
    return jnp.where(
        wavelen < 2048.0, base_rate, jnp.where(wavelen > 8192.0, base_rate / 8.0, blended)
    )


def place(p, b):
    return p ^ (3 * b)


class Spot:
    def __init__(self, p, b, core):
        self.p, self.b, self.core = tuple(p), tuple(b), core

    @staticmethod
    def own():
        sx, sy = lax.axis_index("sx"), lax.axis_index("sy")
        xyz = (sx >> 2, (sy & 1) * 2 + ((sx >> 1) & 1), sy >> 1)
        return Spot([((c + 1) >> 1) & 1 for c in xyz], [c >> 1 for c in xyz], sx & 1)

    @property
    def sx(self):
        ylo = self.p[1] ^ self.b[1]
        return place(self.p[0], self.b[0]) * 4 + ylo * 2 + self.core

    @property
    def sy(self):
        return place(self.p[2], self.b[2]) * 2 + self.b[1]

    @property
    def device(self):
        return (self.sx, self.sy)

    @property
    def chip(self):
        return self.b[0] * 4 + self.b[1] * 2 + self.b[2]

    @property
    def head_block(self):
        return self.chip * 2 + self.core

    @property
    def pair_block(self):
        return (self.b[0] * 2 + self.b[1]) * 2 + self.core

    @property
    def slot(self):
        return self.pair_block * 2 + self.b[2]

    @property
    def part(self):
        return self.p[1] * 2 + self.p[2]

    def member(self, d, dc):
        return Spot(self.p, [b ^ ((d >> s) & 1) for b, s in zip(self.b, (2, 1, 0))], self.core ^ dc)

    def cousin(self, d):
        return Spot([p ^ ((d >> s) & 1) for p, s in zip(self.p, (2, 1, 0))], self.b, self.core)


ORDER = (0, 7, 6, 1, 5, 2, 4, 3)
RELAYS = tuple((0, half, e) for e in (1, 2, 4) for half in range(2)) + (
    (2, 0, 1), (1, 1, 2), (1, 0, 4), (2, 1, 4), (4, 1, 1), (4, 0, 2), (3, 0, 4), (5, 1, 2))


def kernel(q_ref, kv_ref, cos_ref, sin_ref, out_ref,
           qs, qr, kvb, ost, k2, vT, key_place, s0, s1, s2, s3, p0, p1, p2, p3, mx, al, m_ref, acc_ref,
           q_send, q_recv, k1_send, k1_recv, k2_send, k2_recv, f_send, f_recv, o_send, o_recv):
    S, W = (s0, s1, s2, s3), (p0, p1, p2, p3)
    H = CW // 128
    me = Spot.own()
    others = [(d, dc) for d in ORDER for dc in (1, 0) if (d, dc) != (0, 0)]

    def remote(src, dst, send, recv, spot):
        return pltpu.make_async_remote_copy(src_ref=src, dst_ref=dst, send_sem=send, recv_sem=recv, device_id=spot.device, device_id_type=MESH)

    barrier = pltpu.get_barrier_semaphore()
    for d, dc in others:
        pl.semaphore_signal(barrier, inc=1, device_id=me.member(d, dc).device, device_id_type=MESH)
    for d in range(1, 8):
        pl.semaphore_signal(barrier, inc=1, device_id=me.cousin(d).device, device_id_type=MESH)
    pl.semaphore_wait(barrier, len(others) + 7)

    def kv_spot(role, src):
        return kvb.at[role, src.sx, src.part, pl.ds(pl.multiple_of(src.b[2] * 64, 64), 64), :]

    def first(d, dc):
        to = me.member(d, dc)
        return remote(kv_ref.at[to.core, to.chip], kv_spot(to.core, me), k1_send.at[d * 2 + dc], k1_recv.at[me.slot], to)

    for d, dc in others:
        first(d, dc).start()
    kvb[me.core, me.sx, me.part, pl.ds(pl.multiple_of(me.b[2] * 64, 64), 64), :] = kv_ref[me.core, me.chip]

    def queries_to(d, dc):
        to = me.member(d, dc)
        return remote(qs.at[to.head_block], qr.at[me.slot], q_send.at[d * 2 + dc], q_recv.at[me.slot], to)

    for d in ORDER:
        to = me.member(d, 0)
        x = q_ref[:, pl.ds(pl.multiple_of(to.chip * 16, 16), 16), :].astype(F32)
        for c in range(2):
            part = x[:, c * 8:(c + 1) * 8, :].reshape(512, 128)
            turned = part * cos_ref[...] + pltpu.roll(part, 64, 1) * sin_ref[...]
            flat = turned.astype(BF16).T
            for h in range(4):
                qs[to.chip * 2 + c, h] = flat[:, h * 128:(h + 1) * 128]
        for dc in (1, 0):
            if (d, dc) != (0, 0):
                queries_to(d, dc).start()
    qr[me.slot] = qs[me.head_block]

    for d, dc in others:
        frm = me.member(d, dc)
        remote(kv_ref.at[0, 0], kv_spot(me.core, frm), k1_send.at[d * 2 + dc], k1_recv.at[frm.slot], frm).wait_recv()

    def region(spot, half):
        return kvb.at[me.core, pl.ds(pl.multiple_of(place(spot.p[0], half) * 4, 4), 4), spot.part]

    def relay(a, half, e):
        r = region(me.cousin(a), half)
        n = (a ^ e) * 2 + half
        return remote(r, r, k2_send.at[n], k2_recv.at[n], me.cousin(e))

    def forward(d, half):
        r = region(me.cousin(d), half)
        return remote(r, r, f_send.at[d * 2 + half], f_recv.at[d * 2 + half], me.member(0, 1))

    def arrived(d, half):
        r = region(me.cousin(d), half)
        return remote(r, r, k2_send.at[d * 2 + half], k2_recv.at[d * 2 + half], me.cousin(d))

    def handed(d, half):
        r = kvb.at[1 - me.core, pl.ds(pl.multiple_of(place(me.cousin(d).p[0], half) * 4, 4), 4), me.cousin(d).part]
        return remote(r, r, f_send.at[d * 2 + half], f_recv.at[d * 2 + half], me.member(0, 1))

    def pass_on(d):
        for half in range(2):
            arrived(d, half).wait_recv()
            forward(d, half).start()

    for d in (1, 2, 4):
        for half in range(2):
            relay(0, half, d).start()
    for half in range(2):
        forward(0, half).start()

    row = lax.broadcasted_iota(jnp.int32, (KB, 128), 0)
    for ylo in range(2):
        z_at = ((row >> 7) & 1) ^ (3 * ((row >> 6) & 1))
        key_place[ylo] = (z_at * 2 + ((row >> 8) ^ ylo)) * 64 + (row & 63)

    acc_ref[...] = jnp.zeros_like(acc_ref)
    al[...] = jnp.zeros_like(al)
    for w in W[2:]:
        w[...] = jnp.zeros_like(w)

    @pl.loop(0, 16)
    def _(b):
        for h in range(4):
            vT[b, h, 128:VR, :] = jnp.ones((VR - 128, 128), BF16)

    for d in (1, 2):
        pass_on(d)
    for relayed in ((2, 0, 1), (1, 1, 2), (1, 0, 4), (2, 1, 4)):
        relay(*relayed).start()
    pass_on(4)
    for relayed in ((4, 1, 1), (4, 0, 2)):
        relay(*relayed).start()
    pass_on(3)
    relay(3, 0, 4).start()
    for d in range(4):
        for half in range(2):
            handed(d, half).wait_recv()

    px = me.p[0]

    def values_of(half_of):
        @pl.loop(0, 4)
        def _(t):
            b = half_of * 4 + t
            for h in range(4):
                vT[b, h, 0:128, :] = kvb[1, b, h].T
                wide = kvb[0, b, h].astype(F32) * SCALE
                hi = wide.astype(BF16)
                k2[b, 0, pl.ds(h * 128, 128), :] = hi
                k2[b, 1, pl.ds(h * 128, 128), :] = (wide - hi.astype(F32)).astype(BF16)

    values_of(place(px, 0))
    values_of(place(px, 1))

    own_block = me.pair_block

    def early_block(k):
        g = k >> 1
        return own_block ^ (((g + 1) >> 1 & 1) * 4 + (g & 1) * 2 + (k & 1))

    def source(i, bz):
        return Spot(me.p, (i >> 2, (i >> 1) & 1, bz), i & 1)

    def rank(i):
        return (i & 4) + ((me.p[1] ^ ((i >> 1) & 1)) * 2) + (i & 1)

    def early(k, r):
        i = early_block(k)
        b = (px ^ (3 * (r >> 2))) * 4 + (r & 3)
        end = jnp.where(r == rank(i), 1, 0)
        done = end * (1 - (px | (i >> 2)))
        return i + 8 * b + 128 * jnp.where(r == 0, 1, 0) + 256 * done + 512 * end

    def next_early(k, r):
        end = r == rank(early_block(k))
        return jnp.where(end, k + 1, k), jnp.where(end, 0, r + 1)

    def late(v):
        r0, r1 = v & 7, v & 3
        i0 = 4 | ((own_block & 3) ^ (3 - (v >> 3)))
        i1 = early_block(7 - (v >> 2))
        u0 = i0 + 8 * (r0 + 4) + 256 * jnp.where(r0 == 7, 1, 0)
        u1 = i1 + 8 * r1 + 256 * jnp.where(r1 == 3, 1, 0)
        return jnp.where(px == 0, u0, u1)

    def qblock(u):
        return u & 7

    def kblock(u):
        return (u >> 3) & 15

    def queries_in(u):
        @pl.loop(0, (u >> 7) & 1)
        def _(_):
            i = qblock(u)
            for bz in range(2):
                s = 2 * i + bz

                @pl.when(s != me.slot)
                def _():
                    remote(qs.at[0], qr.at[s], q_send.at[0], q_recv.at[s], me.member(1, 0)).wait_recv()

    def qk_stage(u, slot):
        i, b = qblock(u), kblock(u)
        for n in range(QW // CW):
            cols = pl.ds(n * CW, CW)
            kk = jnp.concatenate([k2[b, 0], k2[b, 1]], axis=1)
            qq = jnp.concatenate([qr[2 * i + (n * H + h) // 4, (n * H + h) % 4] for h in range(H)], axis=1)
            qq = jnp.concatenate([qq, qq], axis=0)
            s = jnp.dot(kk, qq, preferred_element_type=F32)
            S[slot][:, cols] = s
            mx[slot, :, cols] = jnp.max(s, axis=0, keepdims=True)

    def mask(u, slot):
        @pl.loop(0, u >> 9)
        def _(_):
            here = source(qblock(u), 0)
            key_at = key_place[me.p[1] ^ here.b[1]]
            lane = lax.broadcasted_iota(jnp.int32, (1, 128), 1) >> 3
            for n in range(QW // 128):
                cols = pl.ds(n * 128, 128)
                query_at = lane + (source(qblock(u), n // 4).sy * 64 + n % 4 * 16)
                s = jnp.where(key_at <= query_at, S[slot][:, cols], NEG)
                S[slot][:, cols] = s
                mx[slot, :, cols] = jnp.max(s, axis=0, keepdims=True)

    def soft_stage(u, slot):
        i = qblock(u)
        m_old = jnp.where((u >> 7) & 1 == 1, NEG, m_ref[i])
        m_new = jnp.maximum(m_old, mx[slot])
        m_ref[i] = m_new
        al[slot] = jnp.exp2(m_old - m_new)
        for n in range(QW // CW):
            cols = pl.ds(n * CW, CW)
            w = jnp.exp2(S[slot][:, cols] - m_new[:, n * CW:(n + 1) * CW]).astype(BF16)
            for h in range(H):
                W[slot][n * H + h] = w[:, h * 128:(h + 1) * 128]

    def pv_stage(u, slot):
        i, b = qblock(u), kblock(u)
        for n in range(QW // CW):
            cols = pl.ds(n * CW, CW)
            ww = jnp.concatenate([W[slot][n * H + h] for h in range(H)], axis=1)
            vv = jnp.concatenate([vT[b, h] for h in range(4)], axis=1)
            acc_ref[i, :, cols] = acc_ref[i, :, cols] * al[slot, :, cols] + jnp.dot(vv, ww, preferred_element_type=F32)

    def outputs_to(s):
        to = Spot(me.p, (s >> 3, (s >> 2) & 1, s & 1), (s >> 1) & 1)
        heads = pl.ds(pl.multiple_of(me.head_block * 8, 8), 8)
        return remote(ost.at[s], out_ref.at[:, heads, :], o_send.at[s], o_recv.at[me.head_block], to)

    def fin(u):
        @pl.loop(0, (u >> 8) & 1)
        def _(_):
            i = qblock(u)
            o = acc_ref[i, 0:128, :] * (1.0 / acc_ref[i, 128:129, :])
            for bz in range(2):
                s = 2 * i + bz
                for t in range(2):
                    c0 = bz * 512 + t * 256
                    ost[s, pl.ds(t * 32, 32)] = o[:, c0:c0 + 256].T.reshape(32, 8, 128).astype(BF16)

                @pl.when(s != me.slot)
                def _():
                    outputs_to(s).start()

                @pl.when(s == me.slot)
                def _():
                    out_ref[:, pl.ds(pl.multiple_of(me.head_block * 8, 8), 8), :] = ost[s]

    def step(old, now, new, cur, nxt):
        if new is not None:
            for n in range(2):
                queries_in(new[n])
            for n in range(2):
                qk_stage(new[n], nxt + n)
        for n in range(2):
            soft_stage(now[n], cur + n)
        for n in range(2):
            pv_stage(old[n], nxt + n)
        if new is not None:
            for n in range(2):
                mask(new[n], nxt + n)
        for n in range(2):
            fin(old[n])

    def take(at):
        k, r = at
        k1, r1 = next_early(k, r)
        return (early(k, r), early(k1, r1)), next_early(k1, r1)

    z = jnp.int32(0)
    u01, at = take((z, z))
    for n in range(2):
        queries_in(u01[n])
        qk_stage(u01[n], n)
        mask(u01[n], n)

    dummy = (u01[0] & 127,) * 2

    def early_steps(t, carry):
        old, now, at = carry
        @pl.loop(0, jnp.where(t == 1, 1, 0))
        def _(_):
            pass_on(5)
            relay(5, 1, 2).start()
            pass_on(6)

        @pl.loop(0, jnp.where(t == 4, 1, 0))
        def _(_):
            pass_on(7)

        new, at = take(at)
        step(old, now, new, 0, 2)
        new2, at = take(at)
        step(now, new, new2, 2, 0)
        return new, new2, at

    old, now, at = lax.fori_loop(0, 8, early_steps, (dummy, u01, at))
    new, _ = take(at)
    step(old, now, new, 0, 2)
    old, now = now, new

    for d in range(4, 8):
        for half in range(2):
            handed(d, half).wait_recv()
    values_of(place(1 - px, 0))
    values_of(place(1 - px, 1))

    def late_steps(t, carry):
        old, now = carry
        new = late(4 * t), late(4 * t + 1)
        step(old, now, new, 2, 0)
        new2 = late(4 * t + 2), late(4 * t + 3)
        step(now, new, new2, 0, 2)
        return new, new2

    old, now = lax.fori_loop(0, 8, late_steps, (old, now))
    step(old, now, None, 2, 0)
    for n in range(2):
        pv_stage(now[n], 2 + n)
    for n in range(2):
        fin(now[n])

    for d, dc in others:
        first(d, dc).wait_send()
        queries_to(d, dc).wait_send()
        frm = me.member(d, dc)
        outputs_to(frm.slot).wait_send()
        heads = pl.ds(pl.multiple_of(frm.head_block * 8, 8), 8)
        remote(ost.at[0], out_ref.at[:, heads, :], o_send.at[frm.slot], o_recv.at[frm.head_block], frm).wait_recv()
    for d in range(8):
        for half in range(2):
            forward(d, half).wait_send()
    for relayed in RELAYS:
        relay(*relayed).wait_send()


def shards(queries, keys, values):
    rows, heads, width = queries.shape
    start = lax.axis_index(("sx", "sy")) * rows
    positions = start + jnp.arange(rows, dtype=jnp.int32)
    angles = positions.astype(F32)[:, None] * frequencies(width)[None, :]
    cosine, sine = jnp.cos(angles), jnp.sin(angles)
    cos2 = jnp.concatenate([cosine, cosine], axis=1)
    sin2 = jnp.concatenate([-sine, sine], axis=1)
    wide = keys.astype(F32)
    turned = wide * cos2[:, None, :] + jnp.roll(wide, width // 2, axis=2) * sin2[:, None, :]
    kv = jnp.stack([turned.astype(BF16).transpose(1, 0, 2), values.transpose(1, 0, 2)])

    def eightfold(a):
        return jnp.broadcast_to(a[:, None, :], (rows, 8, width)).reshape(rows * 8, width)

    dma = pltpu.SemaphoreType.DMA
    return pl.pallas_call(
        kernel,
        out_shape=jax.ShapeDtypeStruct((rows, heads, width), BF16),
        in_specs=[pl.BlockSpec(memory_space=pltpu.VMEM)] * 4,
        out_specs=pl.BlockSpec(memory_space=pltpu.VMEM),
        scratch_shapes=[
            pltpu.VMEM((16, 4, 128, 128), BF16),
            pltpu.VMEM((16, 4, 128, 128), BF16),
            pltpu.VMEM((2, 16, 4, 128, 128), BF16),
            pltpu.VMEM((16, 64, 8, 128), BF16),
            pltpu.VMEM((16, 2, KB, 128), BF16),
            pltpu.VMEM((16, 4, VR, 128), BF16),
            pltpu.VMEM((2, KB, 128), jnp.int32),
            *[pltpu.VMEM((KB, QW), F32)] * 4,
            *[pltpu.VMEM((8, KB, 128), BF16)] * 4,
            pltpu.VMEM((4, 1, QW), F32),
            pltpu.VMEM((4, 1, QW), F32),
            pltpu.VMEM((8, 1, QW), F32),
            pltpu.VMEM((8, VR, QW), F32),
            *[dma((16,))] * 10,
        ],
        compiler_params=pltpu.CompilerParams(
            collective_id=0, has_side_effects=True, vmem_limit_bytes=40 << 20
        ),
        name="fused",
    )(queries, kv, eightfold(cos2), eightfold(sin2))


def solution(mesh):
    placed = P(("sx", "sy"), None, None)
    return jax.shard_map(
        shards, mesh=mesh, in_specs=(placed, placed, placed), out_specs=placed, check_vma=False
    )
```

time: 128 us -> 103 us (0.80); the launches traced: 128 us -> 101 us
  Pallas kernels: 120 us -> 97.2 us
  local copies, waits for them, and re-layouts: 5.67 us -> 2.61 us
    pallas_call x1, Pallas kernels: 120 us -> 97.2 us  [shards(): pl.pallas_call(kernel, out_shape=jax.ShapeDtypeStruct((rows, heads, width...]
    unnamed x4 -> x6, local copies, waits for them, and re-layouts: 4.09 us -> 2.45 us
    reshape x2, local copies, waits for them, and re-layouts: 1.45 us -> 0.04 us  [eightfold(): jnp.broadcast_to(a[:, None, :], (rows, 8, width)).reshape(rows * 8, width)]
where the time goes in v2:
time: 103 us; the launch traced here: 101 us
  Pallas kernels  97.2 us (94%)
  local copies, waits for them, and re-layouts  2.61 us (3%)
  other arithmetic  1.41 us (1%)
    pallas_call x1, Pallas kernels, shards(): pl.pallas_call(kernel, out_shape=jax.ShapeDtypeStruct((rows, heads, width...  97.2 us
    unnamed x6, local copies, waits for them, and re-layouts  2.45 us

profile of v2, /device:TPU:1, one launch (start us, length us, event | category | flops | bytes accessed | tf_op | source)
XLA Modules:
  0.0 101.3 jit_solution(17967089759074232278)
XLA Ops:
  0.0 0.0 copy-start.1
  0.0 0.0 copy-start
  0.0 0.2 multiply_cosine_fusion
  0.2 0.1 pad_maximum_fusion.1
  0.3 1.1 %copy.14 = bf16[64,8,128]{2,0,1:T(8,128)(2,1)S(1)} copy(bf16[64,8,128]{2,1,0:T(8,128)(2,1)} %param.5) | data formatting | bytes 262144 | tf_op args[2]
  1.5 0.9 copy_convert_fusion
  2.4 0.1 fusion.4
  2.6 0.0 copy-done.1
  2.6 0.1 fusion.2
  2.8 0.0 copy-done
  2.8 97.2 %fused.1 = bf16[64,128,128]{2,1,0:T(8,128)(2,1)S(1)} custom-call(bf16[64,128,128]{2,1,0:T(8,128)(2,1)S(1)} %copy-done, bf16[2,8,64,128]{3,2,1,0:T(8,128)(2,1)S(1)} %pad_maximum_fusion.kv_ref, f32[512,128]{1,0:T(8,128)S(1)} %broadcast_bitcast_fusion.1.cos_ref, f32[512,128]{1,0:T(8,128)S(1)} %broadcast_bitcast_fusion.sin_ref), custom_call_target="tpu_custom_call" | custom-call | tf_op jit(solution)/shard_map/fused/pallas_call | solution.py:438
  100.0 1.3 %copy.16 = bf16[64,128,128]{2,1,0:T(8,128)(2,1)} copy(bf16[64,128,128]{2,1,0:T(8,128)(2,1)S(1)} %fused.1) | data formatting | bytes 4194304
  (5 shorter events, 0.1 us)
Async XLA Ops:
  0.0 2.6 %copy-start.1 = (bf16[64,8,128]{2,1,0:T(8,128)(2,1)S(1)}, bf16[64,8,128]{2,1,0:T(8,128)(2,1)}, u32[]{:S(2)}) copy-start(bf16[64,8,128]{2,1,0:T(8,128)(2,1)} %param.4) | copy-start | bytes 393220
  0.0 2.8 %copy-start = (bf16[64,128,128]{2,1,0:T(8,128)(2,1)S(1)}, bf16[64,128,128]{2,1,0:T(8,128)(2,1)}, u32[]{:S(2)}) copy-start(bf16[64,128,128]{2,1,0:T(8,128)(2,1)} %q_ref.1) | copy-start | bytes 6291460

commit v3 on v2

--- a/solution.py
+++ b/solution.py
@@ -84,13 +84,14 @@
         return Spot([p ^ ((d >> s) & 1) for p, s in zip(self.p, (2, 1, 0))], self.b, self.core)
 
 
-ORDER = (0, 7, 6, 1, 5, 2, 4, 3)
+ORDER = (7, 6, 1, 0, 4, 3, 5, 2)
+HEAD_RUNS = 3
 RELAYS = tuple((0, half, e) for e in (1, 2, 4) for half in range(2)) + (
     (2, 0, 1), (1, 1, 2), (1, 0, 4), (2, 1, 4), (4, 1, 1), (4, 0, 2), (3, 0, 4), (5, 1, 2))
 
 
-def kernel(q_ref, kv_ref, cos_ref, sin_ref, out_ref,
-           qs, qr, kvb, ost, k2, vT, key_place, s0, s1, s2, s3, p0, p1, p2, p3, mx, al, m_ref, acc_ref,
+def kernel(q_ref, k_ref, v_ref, cos_ref, sin_ref, out_ref,
+           flat_kv, kv_ref, qs, qr, kvb, ost, k2, vT, key_place, s0, s1, s2, s3, p0, p1, p2, p3, mx, al, m_ref, acc_ref,
            q_send, q_recv, k1_send, k1_recv, k2_send, k2_recv, f_send, f_recv, o_send, o_recv):
     S, W = (s0, s1, s2, s3), (p0, p1, p2, p3)
     H = CW // 128
@@ -105,6 +106,14 @@
         pl.semaphore_signal(barrier, inc=1, device_id=me.member(d, dc).device, device_id_type=MESH)
     for d in range(1, 8):
         pl.semaphore_signal(barrier, inc=1, device_id=me.cousin(d).device, device_id_type=MESH)
+
+    k = k_ref[...].astype(F32).reshape(512, 128)
+    flat_kv[0] = k * cos_ref[...] + pltpu.roll(k, 64, 1) * sin_ref[...]
+    flat_kv[1] = v_ref[...].astype(F32).reshape(512, 128)
+    for role in range(2):
+        for h in range(8):
+            kv_ref[role, h] = flat_kv[role, pl.ds(h, 64, stride=8), :].astype(BF16)
+
     pl.semaphore_wait(barrier, len(others) + 7)
 
     def kv_spot(role, src):
@@ -160,14 +169,14 @@
         r = kvb.at[1 - me.core, pl.ds(pl.multiple_of(place(me.cousin(d).p[0], half) * 4, 4), 4), me.cousin(d).part]
         return remote(r, r, f_send.at[d * 2 + half], f_recv.at[d * 2 + half], me.member(0, 1))
 
-    def pass_on(d):
-        for half in range(2):
-            arrived(d, half).wait_recv()
-            forward(d, half).start()
-
-    for d in (1, 2, 4):
-        for half in range(2):
-            relay(0, half, d).start()
+    def pass_on(d, half, *axes):
+        arrived(d, half).wait_recv()
+        for e in axes:
+            relay(d, half, e).start()
+        forward(d, half).start()
+
+    for e, half in ((1, 1), (2, 0), (4, 1), (1, 0), (2, 1), (4, 0)):
+        relay(0, half, e).start()
     for half in range(2):
         forward(0, half).start()
 
@@ -186,22 +195,21 @@
         for h in range(4):
             vT[b, h, 128:VR, :] = jnp.ones((VR - 128, 128), BF16)
 
-    for d in (1, 2):
-        pass_on(d)
-    for relayed in ((2, 0, 1), (1, 1, 2), (1, 0, 4), (2, 1, 4)):
-        relay(*relayed).start()
-    pass_on(4)
-    for relayed in ((4, 1, 1), (4, 0, 2)):
-        relay(*relayed).start()
-    pass_on(3)
-    relay(3, 0, 4).start()
+    pass_on(2, 0, 1)
+    pass_on(1, 1, 2)
+    pass_on(1, 0, 4)
+    pass_on(2, 1, 4)
+    pass_on(4, 1, 1)
+    pass_on(4, 0, 2)
+    pass_on(3, 0, 4)
+    pass_on(3, 1)
     for d in range(4):
         for half in range(2):
             handed(d, half).wait_recv()
 
     px = me.p[0]
 
-    def values_of(half_of):
+    def keys_of(half_of):
         @pl.loop(0, 4)
         def _(t):
             b = half_of * 4 + t
@@ -212,14 +220,14 @@
                 k2[b, 0, pl.ds(h * 128, 128), :] = hi
                 k2[b, 1, pl.ds(h * 128, 128), :] = (wide - hi.astype(F32)).astype(BF16)
 
-    values_of(place(px, 0))
-    values_of(place(px, 1))
+    keys_of(place(px, 0))
+    keys_of(place(px, 1))
 
     own_block = me.pair_block
 
     def early_block(k):
         g = k >> 1
-        return own_block ^ (((g + 1) >> 1 & 1) * 4 + (g & 1) * 2 + (k & 1))
+        return own_block ^ ((1 - (g & 1)) * 4 + (1 - (g >> 1)) * 2 + (k & 1))
 
     def source(i, bz):
         return Spot(me.p, (i >> 2, (i >> 1) & 1, bz), i & 1)
@@ -227,24 +235,30 @@
     def rank(i):
         return (i & 4) + ((me.p[1] ^ ((i >> 1) & 1)) * 2) + (i & 1)
 
-    def early(k, r):
-        i = early_block(k)
-        b = (px ^ (3 * (r >> 2))) * 4 + (r & 3)
-        end = jnp.where(r == rank(i), 1, 0)
-        done = end * (1 - (px | (i >> 2)))
-        return i + 8 * b + 128 * jnp.where(r == 0, 1, 0) + 256 * done + 512 * end
-
-    def next_early(k, r):
-        end = r == rank(early_block(k))
-        return jnp.where(end, k + 1, k), jnp.where(end, 0, r + 1)
-
-    def late(v):
-        r0, r1 = v & 7, v & 3
-        i0 = 4 | ((own_block & 3) ^ (3 - (v >> 3)))
-        i1 = early_block(7 - (v >> 2))
-        u0 = i0 + 8 * (r0 + 4) + 256 * jnp.where(r0 == 7, 1, 0)
-        u1 = i1 + 8 * r1 + 256 * jnp.where(r1 == 3, 1, 0)
-        return jnp.where(px == 0, u0, u1)
+    def run(n):
+        k = jnp.where(n < HEAD_RUNS, n, jnp.where(n < 2 * HEAD_RUNS, n - HEAD_RUNS, n >> 1))
+        side = jnp.where(n < HEAD_RUNS, 0, jnp.where(n < 2 * HEAD_RUNS, 1, n & 1))
+        return early_block(k), side
+
+    def length(n):
+        i, side = run(n)
+        return jnp.where(side == 0, rank(i) + 1, jnp.where(px == 0, (i & 4) * 2, 4))
+
+    def unit(at):
+        n, r, seen = at
+        i, side = run(n)
+        mine = (px ^ (3 * (r >> 2))) * 4 + (r & 3)
+        other = r + 4 * (1 - px)
+        end = jnp.where(r + 1 == length(n), 1, 0)
+        far = jnp.where(side == 1, 1, 0)
+        done = end * jnp.where(far + (1 - (px | (i >> 2))) > 0, 1, 0)
+        first_of = jnp.where(r == 0, 1, 0) * (1 - far)
+        code = i + 8 * jnp.where(side == 0, mine, other) + 128 * first_of + 256 * done + 512 * end * (1 - far) + 1024 * far * (1 - seen)
+        n1 = n + 1
+        n1 = jnp.where(length(n1) == 0, n1 + 1, n1)
+        n1 = jnp.where(length(n1) == 0, n1 + 1, n1)
+        after = jnp.where(end == 1, jnp.minimum(n1, 15), n), jnp.where(end == 1, 0, r + 1), seen | far
+        return code, after
 
     def qblock(u):
         return u & 7
@@ -263,9 +277,9 @@
                 def _():
                     remote(qs.at[0], qr.at[s], q_send.at[0], q_recv.at[s], me.member(1, 0)).wait_recv()
 
-    def qk_stage(u, slot):
+    def qk_stage(u, slot, pieces=range(QW // CW)):
         i, b = qblock(u), kblock(u)
-        for n in range(QW // CW):
+        for n in pieces:
             cols = pl.ds(n * CW, CW)
             kk = jnp.concatenate([k2[b, 0], k2[b, 1]], axis=1)
             qq = jnp.concatenate([qr[2 * i + (n * H + h) // 4, (n * H + h) % 4] for h in range(H)], axis=1)
@@ -275,7 +289,7 @@
             mx[slot, :, cols] = jnp.max(s, axis=0, keepdims=True)
 
     def mask(u, slot):
-        @pl.loop(0, u >> 9)
+        @pl.loop(0, (u >> 9) & 1)
         def _(_):
             here = source(qblock(u), 0)
             key_at = key_place[me.p[1] ^ here.b[1]]
@@ -287,15 +301,15 @@
                 S[slot][:, cols] = s
                 mx[slot, :, cols] = jnp.max(s, axis=0, keepdims=True)
 
-    def soft_stage(u, slot):
+    def soft_stage(u, slot, pieces=range(QW // CW)):
         i = qblock(u)
-        m_old = jnp.where((u >> 7) & 1 == 1, NEG, m_ref[i])
-        m_new = jnp.maximum(m_old, mx[slot])
-        m_ref[i] = m_new
-        al[slot] = jnp.exp2(m_old - m_new)
-        for n in range(QW // CW):
+        for n in pieces:
             cols = pl.ds(n * CW, CW)
-            w = jnp.exp2(S[slot][:, cols] - m_new[:, n * CW:(n + 1) * CW]).astype(BF16)
+            m_old = jnp.where((u >> 7) & 1 == 1, NEG, m_ref[i, :, cols])
+            m_new = jnp.maximum(m_old, mx[slot, :, cols])
+            m_ref[i, :, cols] = m_new
+            al[slot, :, cols] = jnp.exp2(m_old - m_new)
+            w = jnp.exp2(S[slot][:, cols] - m_new).astype(BF16)
             for h in range(H):
                 W[slot][n * H + h] = w[:, h * 128:(h + 1) * 128]
 
@@ -331,79 +345,90 @@
                 def _():
                     out_ref[:, pl.ds(pl.multiple_of(me.head_block * 8, 8), 8), :] = ost[s]
 
-    def step(old, now, new, cur, nxt):
-        if new is not None:
+    def other_keys(u):
+        @pl.loop(0, (u >> 10) & 1)
+        def _(_):
+            pass_on(7, 0)
+            pass_on(7, 1)
+            for d in range(4, 8):
+                for half in range(2):
+                    handed(d, half).wait_recv()
+            keys_of(place(1 - px, 0))
+            keys_of(place(1 - px, 1))
+
+    def any_of(bits, units):
+        got = units[0] | units[1]
+        return jnp.where((got & bits) != 0, 1, 0)
+
+    def step(old, now, new, at, cur, nxt):
+        if new is None:
+            for n in range(2):
+                soft_stage(now[n], cur + n)
+            for n in range(2):
+                pv_stage(old[n], nxt + n)
+            for n in range(2):
+                fin(old[n])
+            return None
+
+        @pl.loop(0, any_of(128 + 1024, new))
+        def _(_):
             for n in range(2):
                 queries_in(new[n])
-            for n in range(2):
-                qk_stage(new[n], nxt + n)
+                other_keys(new[n])
+
+        ahead, at = take(at)
         for n in range(2):
-            soft_stage(now[n], cur + n)
+            for piece in range(QW // CW):
+                qk_stage(new[n], nxt + n, (piece,))
+                soft_stage(now[n], cur + n, (piece,))
         for n in range(2):
             pv_stage(old[n], nxt + n)
-        if new is not None:
+
+        @pl.loop(0, jnp.maximum(any_of(512, new), any_of(256, old)))
+        def _(_):
             for n in range(2):
                 mask(new[n], nxt + n)
-        for n in range(2):
-            fin(old[n])
+            for n in range(2):
+                fin(old[n])
+
+        return ahead, at
 
     def take(at):
-        k, r = at
-        k1, r1 = next_early(k, r)
-        return (early(k, r), early(k1, r1)), next_early(k1, r1)
+        u, at = unit(at)
+        v, at = unit(at)
+        return (u, v), at
 
     z = jnp.int32(0)
-    u01, at = take((z, z))
+    u01, at = take((z, z, z))
     for n in range(2):
         queries_in(u01[n])
         qk_stage(u01[n], n)
         mask(u01[n], n)
+    new, at = take(at)
 
     dummy = (u01[0] & 127,) * 2
 
-    def early_steps(t, carry):
-        old, now, at = carry
+    def steps(t, carry):
+        old, now, new, at = carry
+
         @pl.loop(0, jnp.where(t == 1, 1, 0))
         def _(_):
-            pass_on(5)
-            relay(5, 1, 2).start()
-            pass_on(6)
-
-        @pl.loop(0, jnp.where(t == 4, 1, 0))
-        def _(_):
-            pass_on(7)
-
-        new, at = take(at)
-        step(old, now, new, 0, 2)
-        new2, at = take(at)
-        step(now, new, new2, 2, 0)
-        return new, new2, at
-
-    old, now, at = lax.fori_loop(0, 8, early_steps, (dummy, u01, at))
-    new, _ = take(at)
-    step(old, now, new, 0, 2)
-    old, now = now, new
-
-    for d in range(4, 8):
-        for half in range(2):
-            handed(d, half).wait_recv()
-    values_of(place(1 - px, 0))
-    values_of(place(1 - px, 1))
-
-    def late_steps(t, carry):
-        old, now = carry
-        new = late(4 * t), late(4 * t + 1)
-        step(old, now, new, 2, 0)
-        new2 = late(4 * t + 2), late(4 * t + 3)
-        step(now, new, new2, 0, 2)
-        return new, new2
-
-    old, now = lax.fori_loop(0, 8, late_steps, (old, now))
-    step(old, now, None, 2, 0)
+            pass_on(5, 1, 2)
+            pass_on(5, 0)
+            pass_on(6, 0)
+            pass_on(6, 1)
+
+        new2, at = step(old, now, new, at, 0, 2)
+        new3, at = step(now, new, new2, at, 2, 0)
+        return new, new2, new3, at
+
+    old, now, new, at = lax.fori_loop(0, 16, steps, (dummy, u01, new, at))
+    step(old, now, new, at, 0, 2)
+    step(now, new, None, None, 2, 0)
     for n in range(2):
-        pv_stage(now[n], 2 + n)
+        pv_stage(new[n], 2 + n)
     for n in range(2):
-        fin(now[n])
+        fin(new[n])
 
     for d, dc in others:
         first(d, dc).wait_send()
@@ -427,10 +452,6 @@
     cosine, sine = jnp.cos(angles), jnp.sin(angles)
     cos2 = jnp.concatenate([cosine, cosine], axis=1)
     sin2 = jnp.concatenate([-sine, sine], axis=1)
-    wide = keys.astype(F32)
-    turned = wide * cos2[:, None, :] + jnp.roll(wide, width // 2, axis=2) * sin2[:, None, :]
-    kv = jnp.stack([turned.astype(BF16).transpose(1, 0, 2), values.transpose(1, 0, 2)])
-
     def eightfold(a):
         return jnp.broadcast_to(a[:, None, :], (rows, 8, width)).reshape(rows * 8, width)
 
@@ -438,9 +459,11 @@
     return pl.pallas_call(
         kernel,
         out_shape=jax.ShapeDtypeStruct((rows, heads, width), BF16),
-        in_specs=[pl.BlockSpec(memory_space=pltpu.VMEM)] * 4,
+        in_specs=[pl.BlockSpec(memory_space=pltpu.VMEM)] * 5,
         out_specs=pl.BlockSpec(memory_space=pltpu.VMEM),
         scratch_shapes=[
+            pltpu.VMEM((2, 512, 128), F32),
+            pltpu.VMEM((2, 8, 64, 128), BF16),
             pltpu.VMEM((16, 4, 128, 128), BF16),
             pltpu.VMEM((16, 4, 128, 128), BF16),
             pltpu.VMEM((2, 16, 4, 128, 128), BF16),
@@ -460,7 +483,7 @@
             collective_id=0, has_side_effects=True, vmem_limit_bytes=40 << 20
         ),
         name="fused",
-    )(queries, kv, eightfold(cos2), eightfold(sin2))
+    )(queries, keys, values, eightfold(cos2), eightfold(sin2))
 
 
 def solution(mesh):

time: 103 us -> 96.5 us (0.937); the launches traced: 101 us -> 96.4 us
  Pallas kernels: 97.2 us -> 91.2 us
  local copies, waits for them, and re-layouts: 2.61 us -> 4.75 us
  other arithmetic: 1.41 us -> 0.31 us
    pallas_call x1, Pallas kernels: 97.2 us -> 91.2 us  [shards(): pl.pallas_call(kernel, out_shape=jax.ShapeDtypeStruct((rows, heads, width...]
    unnamed x6 -> x7, local copies, waits for them, and re-layouts: 2.45 us -> 4.72 us
where the time goes in v3:
time: 96.5 us; the launch traced here: 96.4 us
  Pallas kernels  91.2 us (95%)
  local copies, waits for them, and re-layouts  4.75 us (5%)
    pallas_call x1, Pallas kernels, shards(): pl.pallas_call(kernel, out_shape=jax.ShapeDtypeStruct((rows, heads, width...  91.2 us
    unnamed x7, local copies, waits for them, and re-layouts  4.72 us

profile of v3, /device:TPU:1, one launch (start us, length us, event | category | flops | bytes accessed | tf_op | source)
XLA Modules:
  0.0 96.4 jit_solution(11702015528534849175)
XLA Ops:
  0.0 0.2 fusion
  0.2 0.1 pad_maximum_fusion
  0.4 0.0 copy-start
  0.4 1.6 %copy-done = bf16[64,128,128]{2,1,0:T(8,128)(2,1)S(1)} copy-done((bf16[64,128,128]{2,1,0:T(8,128)(2,1)S(1)}, bf16[64,128,128]{2,1,0:T(8,128)(2,1)}, u32[]{:S(2)}) %copy-start) | copy-done | bytes 2097176
  2.0 0.0 copy-start.1
  2.0 0.9 copy-done.1
  2.9 0.0 copy-start.2
  2.9 0.9 copy-done.2
  3.8 91.2 %fused.1 = bf16[64,128,128]{2,1,0:T(8,128)(2,1)S(1)} custom-call(bf16[64,128,128]{2,1,0:T(8,128)(2,1)S(1)} %copy-done, bf16[64,8,128]{2,1,0:T(8,128)(2,1)S(1)} %copy-done.1, bf16[64,8,128]{2,1,0:T(8,128)(2,1)S(1)} %copy-done.2, f32[512,128]{1,0:T(8,128)S(1)} %broadcast_bitcast_fusion.1.cos_ref, f32[512,128]{1,0:T(8,128)S(1)} %broadcast_bitcast_fusion.sin_ref), custom_call_target="tpu_custom_call" | custom-call | tf_op jit(solution)/shard_map/fused/pallas_call | solution.py:459
  95.0 1.3 %copy.5 = bf16[64,128,128]{2,1,0:T(8,128)(2,1)} copy(bf16[64,128,128]{2,1,0:T(8,128)(2,1)S(1)} %fused.1) | data formatting | bytes 4194304
  (4 shorter events, 0.1 us)
Async XLA Ops:
  0.4 1.6 %copy-start = (bf16[64,128,128]{2,1,0:T(8,128)(2,1)S(1)}, bf16[64,128,128]{2,1,0:T(8,128)(2,1)}, u32[]{:S(2)}) copy-start(bf16[64,128,128]{2,1,0:T(8,128)(2,1)} %q_ref.1) | copy-start | bytes 6291460
  2.0 0.9 copy-start.1
  2.9 0.9 copy-start.2

commit v4 on v3

--- a/solution.py
+++ b/solution.py
@@ -85,13 +85,13 @@
 
 
 ORDER = (7, 6, 1, 0, 4, 3, 5, 2)
-HEAD_RUNS = 3
+HEAD_RUNS = 4
 RELAYS = tuple((0, half, e) for e in (1, 2, 4) for half in range(2)) + (
     (2, 0, 1), (1, 1, 2), (1, 0, 4), (2, 1, 4), (4, 1, 1), (4, 0, 2), (3, 0, 4), (5, 1, 2))
 
 
-def kernel(q_ref, k_ref, v_ref, cos_ref, sin_ref, out_ref,
-           flat_kv, kv_ref, qs, qr, kvb, ost, k2, vT, key_place, s0, s1, s2, s3, p0, p1, p2, p3, mx, al, m_ref, acc_ref,
+def kernel(q_hbm, k_hbm, v_hbm, cos_ref, sin_ref, out_ref,
+           q_ref, k_ref, v_ref, in_sem, flat_kv, kv_ref, qs, qr, kvb, ost, k2, vT, key_place, s0, s1, s2, s3, p0, p1, p2, p3, mx, al, m_ref, acc_ref,
            q_send, q_recv, k1_send, k1_recv, k2_send, k2_recv, f_send, f_recv, o_send, o_recv):
     S, W = (s0, s1, s2, s3), (p0, p1, p2, p3)
     H = CW // 128
@@ -101,12 +101,20 @@
     def remote(src, dst, send, recv, spot):
         return pltpu.make_async_remote_copy(src_ref=src, dst_ref=dst, send_sem=send, recv_sem=recv, device_id=spot.device, device_id_type=MESH)
 
+    inputs = [
+        pltpu.make_async_copy(src, dst, in_sem.at[n])
+        for n, (src, dst) in enumerate(((k_hbm, k_ref), (v_hbm, v_ref), (q_hbm, q_ref)))
+    ]
+    for copy in inputs:
+        copy.start()
     barrier = pltpu.get_barrier_semaphore()
     for d, dc in others:
         pl.semaphore_signal(barrier, inc=1, device_id=me.member(d, dc).device, device_id_type=MESH)
     for d in range(1, 8):
         pl.semaphore_signal(barrier, inc=1, device_id=me.cousin(d).device, device_id_type=MESH)
 
+    for copy in inputs:
+        copy.wait()
     k = k_ref[...].astype(F32).reshape(512, 128)
     flat_kv[0] = k * cos_ref[...] + pltpu.roll(k, 64, 1) * sin_ref[...]
     flat_kv[1] = v_ref[...].astype(F32).reshape(512, 128)
@@ -175,6 +183,23 @@
             relay(d, half, e).start()
         forward(d, half).start()
 
+    def ready(d):
+        for half in range(2):
+            handed(d, half).wait_recv()
+        spot = me.cousin(d)
+        h = spot.part
+
+        @pl.loop(0, 2)
+        def _(t):
+            rows = pl.ds(pl.multiple_of(h * 128, 128), 128)
+            for n in range(4):
+                b = place(spot.p[0], t) * 4 + n
+                vT[b, h, 0:128, :] = kvb[1, b, h].T
+                wide = kvb[0, b, h].astype(F32) * SCALE
+                hi = wide.astype(BF16)
+                k2[b, 0, rows, :] = hi
+                k2[b, 1, rows, :] = (wide - hi.astype(F32)).astype(BF16)
+
     for e, half in ((1, 1), (2, 0), (4, 1), (1, 0), (2, 1), (4, 0)):
         relay(0, half, e).start()
     for half in range(2):
@@ -195,33 +220,21 @@
         for h in range(4):
             vT[b, h, 128:VR, :] = jnp.ones((VR - 128, 128), BF16)
 
+    ready(0)
     pass_on(2, 0, 1)
     pass_on(1, 1, 2)
     pass_on(1, 0, 4)
     pass_on(2, 1, 4)
     pass_on(4, 1, 1)
     pass_on(4, 0, 2)
+    ready(1)
+    ready(2)
     pass_on(3, 0, 4)
     pass_on(3, 1)
-    for d in range(4):
-        for half in range(2):
-            handed(d, half).wait_recv()
+    ready(3)
 
     px = me.p[0]
 
-    def keys_of(half_of):
-        @pl.loop(0, 4)
-        def _(t):
-            b = half_of * 4 + t
-            for h in range(4):
-                vT[b, h, 0:128, :] = kvb[1, b, h].T
-                wide = kvb[0, b, h].astype(F32) * SCALE
-                hi = wide.astype(BF16)
-                k2[b, 0, pl.ds(h * 128, 128), :] = hi
-                k2[b, 1, pl.ds(h * 128, 128), :] = (wide - hi.astype(F32)).astype(BF16)
-
-    keys_of(place(px, 0))
-    keys_of(place(px, 1))
 
     own_block = me.pair_block
 
@@ -332,10 +345,11 @@
             i = qblock(u)
             o = acc_ref[i, 0:128, :] * (1.0 / acc_ref[i, 128:129, :])
             for bz in range(2):
-                s = 2 * i + bz
                 for t in range(2):
                     c0 = bz * 512 + t * 256
-                    ost[s, pl.ds(t * 32, 32)] = o[:, c0:c0 + 256].T.reshape(32, 8, 128).astype(BF16)
+                    ost[2 * i + bz, pl.ds(t * 32, 32)] = o[:, c0:c0 + 256].T.reshape(32, 8, 128).astype(BF16)
+            for bz in range(2):
+                s = 2 * i + bz
 
                 @pl.when(s != me.slot)
                 def _():
@@ -351,10 +365,7 @@
             pass_on(7, 0)
             pass_on(7, 1)
             for d in range(4, 8):
-                for half in range(2):
-                    handed(d, half).wait_recv()
-            keys_of(place(1 - px, 0))
-            keys_of(place(1 - px, 1))
+                ready(d)
 
     def any_of(bits, units):
         got = units[0] | units[1]
@@ -459,9 +470,13 @@
     return pl.pallas_call(
         kernel,
         out_shape=jax.ShapeDtypeStruct((rows, heads, width), BF16),
-        in_specs=[pl.BlockSpec(memory_space=pltpu.VMEM)] * 5,
+        in_specs=[pl.BlockSpec(memory_space=pltpu.HBM)] * 3 + [pl.BlockSpec(memory_space=pltpu.VMEM)] * 2,
         out_specs=pl.BlockSpec(memory_space=pltpu.VMEM),
         scratch_shapes=[
+            pltpu.VMEM((rows, heads, width), BF16),
+            pltpu.VMEM((rows, 8, width), BF16),
+            pltpu.VMEM((rows, 8, width), BF16),
+            dma((3,)),
             pltpu.VMEM((2, 512, 128), F32),
             pltpu.VMEM((2, 8, 64, 128), BF16),
             pltpu.VMEM((16, 4, 128, 128), BF16),
@@ -483,7 +498,11 @@
             collective_id=0, has_side_effects=True, vmem_limit_bytes=40 << 20
         ),
         name="fused",
-    )(queries, keys, values, eightfold(cos2), eightfold(sin2))
+    )(
+        *(pltpu.with_memory_space_constraint(a, pltpu.HBM) for a in (queries, keys, values)),
+        eightfold(cos2),
+        eightfold(sin2),
+    )
 
 
 def solution(mesh):

time: 96.5 us -> 92.7 us (0.961)
  local copies, waits for them, and re-layouts: 4.75 us -> 1.36 us
    unnamed x7 -> x1, local copies, waits for them, and re-layouts: 4.72 us -> 1.32 us
where the time goes in v4:
time: 92.7 us; the launch traced here: 92.6 us
  Pallas kernels  90.9 us (98%)
  local copies, waits for them, and re-layouts  1.36 us (1%)
    pallas_call x1, Pallas kernels, shards(): pl.pallas_call(kernel, out_shape=jax.ShapeDtypeStruct((rows, heads, width...  90.9 us

profile of v4, /device:TPU:1, one launch (start us, length us, event | category | flops | bytes accessed | tf_op | source)
XLA Modules:
  0.0 92.6 jit_solution(8309985626731685717)
XLA Ops:
  0.0 0.2 fusion
  0.2 0.1 pad_maximum_fusion
  0.4 90.9 %fused.1 = bf16[64,128,128]{2,1,0:T(8,128)(2,1)S(1)} custom-call(bf16[64,128,128]{2,1,0:T(8,128)(2,1)} %q_hbm.1, bf16[64,8,128]{2,1,0:T(8,128)(2,1)} %k_hbm.1, bf16[64,8,128]{2,1,0:T(8,128)(2,1)} %v_hbm.1, f32[512,128]{1,0:T(8,128)S(1)} %broadcast_bitcast_fusion.1.cos_ref, f32[512,128]{1,0:T(8,128)S(1)} %broadcast_bitcast_fusion.sin_ref), custom_call_target="tpu_custom_call" | custom-call | tf_op jit(solution)/shard_map/fused/pallas_call | solution.py:470
  91.3 1.3 %copy.5 = bf16[64,128,128]{2,1,0:T(8,128)(2,1)} copy(bf16[64,128,128]{2,1,0:T(8,128)(2,1)S(1)} %fused.1) | data formatting | bytes 4194304
  (4 shorter events, 0.1 us)

commit v5 on v4

--- a/solution.py
+++ b/solution.py
@@ -85,6 +85,7 @@
 
 
 ORDER = (7, 6, 1, 0, 4, 3, 5, 2)
+AHEAD = 4
 HEAD_RUNS = 4
 RELAYS = tuple((0, half, e) for e in (1, 2, 4) for half in range(2)) + (
     (2, 0, 1), (1, 1, 2), (1, 0, 4), (2, 1, 4), (4, 1, 1), (4, 0, 2), (3, 0, 4), (5, 1, 2))
@@ -113,6 +114,21 @@
     for d in range(1, 8):
         pl.semaphore_signal(barrier, inc=1, device_id=me.cousin(d).device, device_id_type=MESH)
 
+    row = lax.broadcasted_iota(jnp.int32, (KB, 128), 0)
+    for ylo in range(2):
+        z_at = ((row >> 7) & 1) ^ (3 * ((row >> 6) & 1))
+        key_place[ylo] = (z_at * 2 + ((row >> 8) ^ ylo)) * 64 + (row & 63)
+
+    acc_ref[...] = jnp.zeros_like(acc_ref)
+    al[...] = jnp.zeros_like(al)
+    for w in W[2:]:
+        w[...] = jnp.zeros_like(w)
+
+    @pl.loop(0, 16)
+    def _(b):
+        for h in range(4):
+            vT[b, h, 128:VR, :] = jnp.ones((VR - 128, 128), BF16)
+
     for copy in inputs:
         copy.wait()
     k = k_ref[...].astype(F32).reshape(512, 128)
@@ -122,24 +138,7 @@
         for h in range(8):
             kv_ref[role, h] = flat_kv[role, pl.ds(h, 64, stride=8), :].astype(BF16)
 
-    pl.semaphore_wait(barrier, len(others) + 7)
-
-    def kv_spot(role, src):
-        return kvb.at[role, src.sx, src.part, pl.ds(pl.multiple_of(src.b[2] * 64, 64), 64), :]
-
-    def first(d, dc):
-        to = me.member(d, dc)
-        return remote(kv_ref.at[to.core, to.chip], kv_spot(to.core, me), k1_send.at[d * 2 + dc], k1_recv.at[me.slot], to)
-
-    for d, dc in others:
-        first(d, dc).start()
-    kvb[me.core, me.sx, me.part, pl.ds(pl.multiple_of(me.b[2] * 64, 64), 64), :] = kv_ref[me.core, me.chip]
-
-    def queries_to(d, dc):
-        to = me.member(d, dc)
-        return remote(qs.at[to.head_block], qr.at[me.slot], q_send.at[d * 2 + dc], q_recv.at[me.slot], to)
-
-    for d in ORDER:
+    def rotate_for(d):
         to = me.member(d, 0)
         x = q_ref[:, pl.ds(pl.multiple_of(to.chip * 16, 16), 16), :].astype(F32)
         for c in range(2):
@@ -148,6 +147,29 @@
             flat = turned.astype(BF16).T
             for h in range(4):
                 qs[to.chip * 2 + c, h] = flat[:, h * 128:(h + 1) * 128]
+
+    for d in ORDER[:AHEAD]:
+        rotate_for(d)
+    pl.semaphore_wait(barrier, len(others) + 7)
+
+    def kv_spot(role, src):
+        return kvb.at[role, src.sx, src.part, pl.ds(pl.multiple_of(src.b[2] * 64, 64), 64), :]
+
+    def first(d, dc):
+        to = me.member(d, dc)
+        return remote(kv_ref.at[to.core, to.chip], kv_spot(to.core, me), k1_send.at[d * 2 + dc], k1_recv.at[me.slot], to)
+
+    for d, dc in others:
+        first(d, dc).start()
+    kvb[me.core, me.sx, me.part, pl.ds(pl.multiple_of(me.b[2] * 64, 64), 64), :] = kv_ref[me.core, me.chip]
+
+    def queries_to(d, dc):
+        to = me.member(d, dc)
+        return remote(qs.at[to.head_block], qr.at[me.slot], q_send.at[d * 2 + dc], q_recv.at[me.slot], to)
+
+    for n, d in enumerate(ORDER):
+        if n >= AHEAD:
+            rotate_for(d)
         for dc in (1, 0):
             if (d, dc) != (0, 0):
                 queries_to(d, dc).start()
@@ -204,21 +226,6 @@
         relay(0, half, e).start()
     for half in range(2):
         forward(0, half).start()
-
-    row = lax.broadcasted_iota(jnp.int32, (KB, 128), 0)
-    for ylo in range(2):
-        z_at = ((row >> 7) & 1) ^ (3 * ((row >> 6) & 1))
-        key_place[ylo] = (z_at * 2 + ((row >> 8) ^ ylo)) * 64 + (row & 63)
-
-    acc_ref[...] = jnp.zeros_like(acc_ref)
-    al[...] = jnp.zeros_like(al)
-    for w in W[2:]:
-        w[...] = jnp.zeros_like(w)
-
-    @pl.loop(0, 16)
-    def _(b):
-        for h in range(4):
-            vT[b, h, 128:VR, :] = jnp.ones((VR - 128, 128), BF16)
 
     ready(0)
     pass_on(2, 0, 1)
@@ -422,7 +429,7 @@
     def steps(t, carry):
         old, now, new, at = carry
 
-        @pl.loop(0, jnp.where(t == 1, 1, 0))
+        @pl.loop(0, jnp.where(t == 2, 1, 0))
         def _(_):
             pass_on(5, 1, 2)
             pass_on(5, 0)

time: 92.7 us -> 92 us (level)
  no operation moved by 1% of the time
where the time goes in v5:
time: 92 us; the launch traced here: 91.8 us
  Pallas kernels  90.1 us (98%)
  local copies, waits for them, and re-layouts  1.36 us (1%)
    pallas_call x1, Pallas kernels, shards(): pl.pallas_call(kernel, out_shape=jax.ShapeDtypeStruct((rows, heads, width...  90.1 us

profile of v5, /device:TPU:1, one launch (start us, length us, event | category | flops | bytes accessed | tf_op | source)
XLA Modules:
  0.0 91.8 jit_solution(15236880339190708421)
XLA Ops:
  0.0 0.2 fusion
  0.2 0.1 pad_maximum_fusion
  0.4 90.1 %fused.1 = bf16[64,128,128]{2,1,0:T(8,128)(2,1)S(1)} custom-call(bf16[64,128,128]{2,1,0:T(8,128)(2,1)} %q_hbm.1, bf16[64,8,128]{2,1,0:T(8,128)(2,1)} %k_hbm.1, bf16[64,8,128]{2,1,0:T(8,128)(2,1)} %v_hbm.1, f32[512,128]{1,0:T(8,128)S(1)} %broadcast_bitcast_fusion.1.cos_ref, f32[512,128]{1,0:T(8,128)S(1)} %broadcast_bitcast_fusion.sin_ref), custom_call_target="tpu_custom_call" | custom-call | tf_op jit(solution)/shard_map/fused/pallas_call | solution.py:477
  90.5 1.3 %copy.5 = bf16[64,128,128]{2,1,0:T(8,128)(2,1)} copy(bf16[64,128,128]{2,1,0:T(8,128)(2,1)S(1)} %fused.1) | data formatting | bytes 4194304
  (4 shorter events, 0.1 us)

commit v6 on v5

--- a/solution.py
+++ b/solution.py
@@ -111,7 +111,7 @@
     barrier = pltpu.get_barrier_semaphore()
     for d, dc in others:
         pl.semaphore_signal(barrier, inc=1, device_id=me.member(d, dc).device, device_id_type=MESH)
-    for d in range(1, 8):
+    for d in (1, 2, 4):
         pl.semaphore_signal(barrier, inc=1, device_id=me.cousin(d).device, device_id_type=MESH)
 
     row = lax.broadcasted_iota(jnp.int32, (KB, 128), 0)
@@ -150,7 +150,7 @@
 
     for d in ORDER[:AHEAD]:
         rotate_for(d)
-    pl.semaphore_wait(barrier, len(others) + 7)
+    pl.semaphore_wait(barrier, len(others) + 3)
 
     def kv_spot(role, src):
         return kvb.at[role, src.sx, src.part, pl.ds(pl.multiple_of(src.b[2] * 64, 64), 64), :]
@@ -211,16 +211,14 @@
         spot = me.cousin(d)
         h = spot.part
 
-        @pl.loop(0, 2)
-        def _(t):
-            rows = pl.ds(pl.multiple_of(h * 128, 128), 128)
-            for n in range(4):
-                b = place(spot.p[0], t) * 4 + n
-                vT[b, h, 0:128, :] = kvb[1, b, h].T
-                wide = kvb[0, b, h].astype(F32) * SCALE
-                hi = wide.astype(BF16)
-                k2[b, 0, rows, :] = hi
-                k2[b, 1, rows, :] = (wide - hi.astype(F32)).astype(BF16)
+        rows = pl.ds(pl.multiple_of(h * 128, 128), 128)
+        for n in range(8):
+            b = place(spot.p[0], n // 4) * 4 + n % 4
+            vT[b, h, 0:128, :] = kvb[1, b, h].T
+            wide = kvb[0, b, h].astype(F32) * SCALE
+            hi = wide.astype(BF16)
+            k2[b, 0, rows, :] = hi
+            k2[b, 1, rows, :] = (wide - hi.astype(F32)).astype(BF16)
 
     for e, half in ((1, 1), (2, 0), (4, 1), (1, 0), (2, 1), (4, 0)):
         relay(0, half, e).start()

time: 92 us -> 91.6 us (level)
  no operation moved by 1% of the time
where the time goes in v6:
time: 91.6 us; the launch traced here: 91.5 us
  Pallas kernels  89.8 us (98%)
  local copies, waits for them, and re-layouts  1.36 us (1%)
    pallas_call x1, Pallas kernels, shards(): pl.pallas_call(kernel, out_shape=jax.ShapeDtypeStruct((rows, heads, width...  89.8 us

profile of v6, /device:TPU:1, one launch (start us, length us, event | category | flops | bytes accessed | tf_op | source)
XLA Modules:
  0.0 91.5 jit_solution(16676850476478094407)
XLA Ops:
  0.0 0.2 fusion
  0.2 0.1 pad_maximum_fusion
  0.4 89.8 %fused.1 = bf16[64,128,128]{2,1,0:T(8,128)(2,1)S(1)} custom-call(bf16[64,128,128]{2,1,0:T(8,128)(2,1)} %q_hbm.1, bf16[64,8,128]{2,1,0:T(8,128)(2,1)} %k_hbm.1, bf16[64,8,128]{2,1,0:T(8,128)(2,1)} %v_hbm.1, f32[512,128]{1,0:T(8,128)S(1)} %broadcast_bitcast_fusion.1.cos_ref, f32[512,128]{1,0:T(8,128)S(1)} %broadcast_bitcast_fusion.sin_ref), custom_call_target="tpu_custom_call" | custom-call | tf_op jit(solution)/shard_map/fused/pallas_call | solution.py:475
  90.2 1.3 %copy.5 = bf16[64,128,128]{2,1,0:T(8,128)(2,1)} copy(bf16[64,128,128]{2,1,0:T(8,128)(2,1)S(1)} %fused.1) | data formatting | bytes 4194304
  (4 shorter events, 0.1 us)
